TPU v7x, 32 devices: a whole 2x2x4 slice. The times are simulated.
32 devices in a mesh: rows: 8 (over z, y), cols: 4 (over x, core).
Axes of the slice: x: 2, y: 2, z: 4, core: 2. Of those that a mesh axis runs over, the one named last changes fastest.
Arguments:
- points: bfloat16 [4096, 256], P(('rows', 'cols')), may hold values from -6 to 6
- start_vectors: float32 [8, 4096], P(None, ('rows', 'cols')), may hold values from -6 to 6
- degree: bfloat16 [4096], P(('rows', 'cols')), may hold values from 0.19921875 to 2
Outputs:
- embedding: float32 [8, 4096], P(None, ('rows', 'cols'))
All inputs are finite; a program needn't handle non-finite values.
Results may differ from a plain program's by a relative error of at most 0.0034.
Values may be sent and summed in bfloat16 or wider, within the bound.
No kernel may reach another device: no remote copies, remote signals or barrier semaphores. Data moves between devices by JAX's collectives and lax.ppermute only.
A program may use at most 64 MiB of HBM per device.

v0:
```python
import jax
import jax.numpy as jnp
from jax import lax
from jax.sharding import PartitionSpec as P

ITERS = 3


def body(points, start_vectors, degree):
    row_count = lax.axis_size("rows")
    col_count = lax.axis_size("cols")
    row_place = lax.axis_index("rows")
    col_place = lax.axis_index("cols")
    span_size = points.shape[0]
    sharpness = 4.0 / points.shape[1]
    row_points, row_degree = (
        lax.all_gather(points, "cols", axis=0, tiled=True),
        lax.all_gather(degree, "cols", axis=0, tiled=True),
    )
    row_total = row_points.shape[0]
    row_float = row_points.astype(jnp.float32)
    row_norms = jnp.sum(row_float * row_float, axis=1)
    row_slots = jnp.arange(row_total, dtype=jnp.int32)
    row_global = (
        row_place * col_count + row_slots // span_size
    ) * span_size + row_slots % span_size

    def kernel_block(x_block, col_norms, first_slot):
        inner = lax.dot_general(
            row_points, x_block, (((1,), (1,)), ((), ())), preferred_element_type=jnp.float32
        )
        distance = row_norms[:, None] + col_norms[None, :] - 2.0 * inner
        kernel = jnp.exp(-sharpness * distance)
        col_slots = first_slot + jnp.arange(x_block.shape[0], dtype=jnp.int32)
        col_global = (
            col_slots // span_size * col_count + col_place
        ) * span_size + col_slots % span_size
        return jnp.where(
            row_global[:, None] == col_global[None, :], jnp.float32(0.0), kernel
        ).astype(jnp.bfloat16)

    vectors = start_vectors
    for iteration in range(ITERS):
        empty = jnp.zeros((vectors.shape[0], row_total), jnp.float32)
        sending = vectors.T.astype(jnp.bfloat16)
        x_piece = lax.all_gather(points, "rows", axis=0, tiled=True)
        v_piece = lax.all_gather(sending, "rows", axis=0, tiled=True)
        piece_rows = x_piece.shape[0]
        block_size = 512
        block_count = piece_rows // block_size

        def accumulate(block_index, running):
            offset = block_index * block_size
            x_block = lax.dynamic_slice_in_dim(x_piece, offset, block_size, 0)
            v_block = lax.dynamic_slice_in_dim(v_piece, offset, block_size, 0)
            x_float = x_block.astype(jnp.float32)
            col_norms = jnp.sum(x_float * x_float, axis=1)
            kernel = kernel_block(x_block, col_norms, offset)
            return running + lax.dot_general(
                v_block, kernel, (((0,), (1,)), ((), ())), preferred_element_type=jnp.float32
            )

        partial_value = lax.fori_loop(0, block_count, accumulate, empty)
        summed = lax.psum(partial_value, "cols")
        row_state = summed / row_degree.astype(jnp.float32)[None, :]
        vectors = lax.dynamic_slice_in_dim(row_state, col_place * span_size, span_size, 1)
    magnitude = lax.psum(jnp.sum(jnp.abs(row_state), axis=1), "rows")
    mean_abs = magnitude / (span_size * row_count * col_count)
    return vectors / (mean_abs[:, None] + 1e-06)


def solution(mesh):
    return jax.shard_map(
        body,
        mesh=mesh,
        in_specs=(P(("rows", "cols"), None), P(None, ("rows", "cols")), P(("rows", "cols"))),
        out_specs=P(None, ("rows", "cols")),
        check_vma=False,
    )
```

profile of v0, /device:TPU:0, one launch (start us, length us, event | category | flops | bytes accessed | tf_op | source)
XLA Modules:
  0.0 177.6 jit_solution(2372064318550203494)
XLA Ops:
  0.0 0.7 copy-done.2
  0.7 6.0 %all-gather = bf16[4,1,128]{2,1,0:T(2,128)(2,1)S(1)} all-gather(bf16[1,1,128]{2,1,0:T(2,128)(2,1)S(1)} %bitcast.73), channel_id=1, replica_groups=mesh['rows'=8,'cols'=4] {'cols'}, dimensions={0}, use_global_device_ids=true | all-gather | bytes 1280 | tf_op jit(solution)/shard_map/all_gather | solution.py:18
  6.7 0.1 dynamic-slice
  6.7 6.5 %all_gather.21 = bf16[512,256]{1,0:T(8,128)(2,1)S(1)} all-gather(bf16[128,256]{1,0:T(8,128)(2,1)} %param.9), channel_id=1, replica_groups=mesh['rows'=8,'cols'=4] {'cols'}, dimensions={0}, use_global_device_ids=true | all-gather | bytes 327680 | tf_op jit(solution)/shard_map/all_gather | solution.py:17
  13.2 0.1 multiply_reduce_fusion.3
  13.4 0.7 copy-done
  14.0 32.1 %all_gather.22 = bf16[1024,256]{1,0:T(8,128)(2,1)S(1)} all-gather(bf16[128,256]{1,0:T(8,128)(2,1)S(1)} %copy-done), channel_id=1, replica_groups=mesh['rows'=8,'cols'=4] {'rows'}, dimensions={0}, use_global_device_ids=true | all-gather | bytes 589824 | tf_op jit(solution)/shard_map/all_gather | solution.py:46
  46.2 0.0 copy-done.1
  46.2 26.1 %all_gather.20 = bf16[1024,8]{0,1:T(8,128)(2,1)S(1)} all-gather(bf16[128,8]{0,1:T(8,128)(2,1)S(1)} %convert_bitcast_fusion), channel_id=1, replica_groups=mesh['rows'=8,'cols'=4] {'rows'}, dimensions={0}, use_global_device_ids=true | all-gather | bytes 18432 | tf_op jit(solution)/shard_map/all_gather | solution.py:47
  72.3 1.6 while.48
  72.3 0.1 multiply_reduce_fusion.7
  72.5 0.6 fusion.155
  73.1 0.2 multiply_reduce_fusion.7
  73.3 0.6 fusion.155
  73.9 10.1 %psum.28 = f32[8,512]{1,0:T(8,128)S(1)} all-reduce(f32[8,512]{1,0:T(8,128)S(1)} %get-tuple-element.608), channel_id=1, replica_groups=mesh['rows'=8,'cols'=4] {'cols'}, use_global_device_ids=true, to_apply=%region_4.5 | all-reduce | flops 4096 | bytes 32768 | tf_op jit(solution)/shard_map/psum | solution.py:64
  84.0 26.1 %all_gather.24 = bf16[1024,8]{0,1:T(8,128)(2,1)S(1)} all-gather(bf16[128,8]{0,1:T(8,128)(2,1)S(1)} %fusion.131), channel_id=1, replica_groups=mesh['rows'=8,'cols'=4] {'rows'}, dimensions={0}, use_global_device_ids=true | all-gather | bytes 18432 | tf_op jit(solution)/shard_map/all_gather | solution.py:47
  110.1 1.6 while.49
  110.1 0.1 multiply_reduce_fusion.8
  110.3 0.6 fusion.160
  110.9 0.2 multiply_reduce_fusion.8
  111.1 0.6 fusion.160
  111.7 10.1 %psum.29 = f32[8,512]{1,0:T(8,128)S(1)} all-reduce(f32[8,512]{1,0:T(8,128)S(1)} %get-tuple-element.609), channel_id=1, replica_groups=mesh['rows'=8,'cols'=4] {'cols'}, use_global_device_ids=true, to_apply=%region_8.9 | all-reduce | flops 4096 | bytes 32768 | tf_op jit(solution)/shard_map/psum | solution.py:64
  121.8 26.1 %all_gather.25 = bf16[1024,8]{0,1:T(8,128)(2,1)S(1)} all-gather(bf16[128,8]{0,1:T(8,128)(2,1)S(1)} %fusion.132), channel_id=1, replica_groups=mesh['rows'=8,'cols'=4] {'rows'}, dimensions={0}, use_global_device_ids=true | all-gather | bytes 18432 | tf_op jit(solution)/shard_map/all_gather | solution.py:47
  148.0 1.6 while.50
  148.0 0.1 multiply_reduce_fusion.9
  148.1 0.6 fusion.165
  148.7 0.2 multiply_reduce_fusion.9
  148.9 0.6 fusion.165
  149.5 10.1 %psum.30 = f32[8,512]{1,0:T(8,128)S(1)} all-reduce(f32[8,512]{1,0:T(8,128)S(1)} %get-tuple-element.610), channel_id=1, replica_groups=mesh['rows'=8,'cols'=4] {'cols'}, use_global_device_ids=true, to_apply=%region_12.13 | all-reduce | flops 4096 | bytes 32768 | tf_op jit(solution)/shard_map/psum | solution.py:64
  159.7 0.1 abs_reduce_fusion
  159.8 17.1 %psum.31 = f32[8]{0:T(128)S(1)} all-reduce(f32[8]{0:T(128)S(1)} %get-tuple-element.749), channel_id=1, replica_groups=mesh['rows'=8,'cols'=4] {'rows'}, use_global_device_ids=true, to_apply=%region_14.15 | all-reduce | flops 8 | bytes 64 | tf_op jit(solution)/shard_map/psum | solution.py:67
  176.9 0.7 dynamic-slice_divide_fusion.2
  (17 shorter events, 0.1 us)
Async XLA Ops:
  0.0 0.7 copy-start.2
  13.2 0.8 copy-start
  14.0 32.1 %copy-start.1 = (f32[8,128]{1,0:T(8,128)S(1)}, f32[8,128]{1,0:T(8,128)}, u32[]{:S(2)}) copy-start(f32[8,128]{1,0:T(8,128)} %param.10) | copy-start | bytes 12292
where the time goes:
time: 178 us
  blocking collectives  170 us (96%)
  matrix products  3.57 us (2%)
  other arithmetic  2.03 us (1%)
    all_gather x3, blocking collectives, body(): v_piece = lax.all_gather(sending, 'rows', axis=0, tiled=True)  78.3 us
    all_gather x1, blocking collectives, body(): x_piece = lax.all_gather(points, 'rows', axis=0, tiled=True)  32.1 us
    psum x3, blocking collectives, body(): summed = lax.psum(partial_value, 'cols')  30.4 us
    psum x1, blocking collectives, body(): magnitude = lax.psum(jnp.sum(jnp.abs(row_state), axis=1), 'rows')  17.1 us
    all_gather x1, blocking collectives, body(): lax.all_gather(points, 'cols', axis=0, tiled=True)  6.47 us
    all_gather x1, blocking collectives, body(): lax.all_gather(degree, 'cols', axis=0, tiled=True)  5.99 us
    dot_general x6, matrix products, accumulate(): lax.dot_general(v_block, kernel, (((0,), (1,)), ((), ())), preferred_elem...  3.57 us

commit v1 on v0

--- a/solution.py
+++ b/solution.py
@@ -6,7 +6,7 @@
 ITERS = 3
 
 
-def body(points, start_vectors, degree):
+def general(points, start_vectors, degree):
     row_count = lax.axis_size("rows")
     col_count = lax.axis_size("cols")
     row_place = lax.axis_index("rows")
@@ -24,6 +24,7 @@
     row_global = (
         row_place * col_count + row_slots // span_size
     ) * span_size + row_slots % span_size
+    x_piece = lax.all_gather(points, "rows", axis=0, tiled=True)
 
     def kernel_block(x_block, col_norms, first_slot):
         inner = lax.dot_general(
@@ -43,10 +44,9 @@
     for iteration in range(ITERS):
         empty = jnp.zeros((vectors.shape[0], row_total), jnp.float32)
         sending = vectors.T.astype(jnp.bfloat16)
-        x_piece = lax.all_gather(points, "rows", axis=0, tiled=True)
         v_piece = lax.all_gather(sending, "rows", axis=0, tiled=True)
         piece_rows = x_piece.shape[0]
-        block_size = 512
+        block_size = span_size * min(4, row_count)
         block_count = piece_rows // block_size
 
         def accumulate(block_index, running):
@@ -69,9 +69,92 @@
     return vectors / (mean_abs[:, None] + 1e-06)
 
 
+def swap(value, axis, bit):
+    count = lax.axis_size(axis)
+    return lax.ppermute(value, axis, [(place, place ^ bit) for place in range(count)])
+
+
+def planes(points, start_vectors, degree):
+    row_count = lax.axis_size("rows")
+    span, features = points.shape
+    vector_count = start_vectors.shape[0]
+    sharpness = 4.0 / features
+    extra = jnp.concatenate(
+        [
+            start_vectors.astype(jnp.bfloat16),
+            jnp.broadcast_to(degree[None, :], (vector_count, span)),
+        ],
+        axis=1,
+    )
+    message = jnp.concatenate([points, extra], axis=0)
+    pieces = [message] + [swap(message, "rows", bit) for bit in range(2, row_count, 2)]
+    own = jnp.stack(pieces)
+    by_x = swap(own, "cols", 2)
+    by_y = swap(own, "rows", 1)
+    by_core = swap(own, "cols", 1)
+    by_x_core = swap(by_x, "cols", 1)
+
+    def unpack(parts):
+        whole = jnp.concatenate(parts, axis=0)
+        x = whole[:, :span, :].reshape(-1, features)
+        v = jnp.transpose(whole[:, span:, :span], (1, 0, 2)).reshape(vector_count, -1)
+        d = whole[:, span, span:].reshape(1, -1)
+        return x, v, d.astype(jnp.float32)
+
+    row_x, row_v, row_degree = unpack([own, by_x, by_core, by_x_core])
+    col_x, _, col_degree = unpack([own, by_y])
+
+    def norms(x):
+        f = x.astype(jnp.float32)
+        return jnp.sum(f * f, axis=1)
+
+    inner = lax.dot_general(
+        row_x, col_x, (((1,), (1,)), ((), ())), preferred_element_type=jnp.float32
+    )
+    distance = norms(row_x)[:, None] + norms(col_x)[None, :] - 2.0 * inner
+    kernel = jnp.exp(-sharpness * distance)
+    row_slot = jnp.arange(row_x.shape[0], dtype=jnp.int32)
+    col_slot = jnp.arange(col_x.shape[0], dtype=jnp.int32)
+    block = own.shape[0] * span
+    diagonal = (row_slot[:, None] == col_slot[None, :]) & (row_slot < block)[:, None]
+    kernel = jnp.where(diagonal, jnp.float32(0.0), kernel).astype(jnp.bfloat16)
+    kernel = lax.optimization_barrier(kernel)
+
+    def to_cols(v):
+        part = lax.dot_general(
+            v, kernel, (((1,), (0,)), ((), ())), preferred_element_type=jnp.float32
+        )
+        other = swap(part, "rows", 1)
+        other = jnp.concatenate([other[:, block:], other[:, :block]], axis=1)
+        return (part + other) / col_degree
+
+    def to_rows(v):
+        part = lax.dot_general(
+            v, kernel, (((1,), (1,)), ((), ())), preferred_element_type=jnp.float32
+        )
+        other = swap(part, "cols", 1)
+        part = part + jnp.concatenate([other[:, 2 * block :], other[:, : 2 * block]], axis=1)
+        other = swap(part, "cols", 3)
+        part = part + jnp.concatenate(
+            [other[:, at * block : (at + 1) * block] for at in (3, 2, 1, 0)], axis=1
+        )
+        return part / row_degree
+
+    state = to_cols(row_v)
+    state = to_rows(state.astype(jnp.bfloat16))
+    state = to_cols(state.astype(jnp.bfloat16))
+    magnitude = jnp.sum(jnp.abs(state), axis=1, keepdims=True)
+    magnitude = jnp.broadcast_to(magnitude, (vector_count, span))
+    magnitude = magnitude + swap(magnitude, "cols", 1)
+    magnitude = magnitude + swap(magnitude, "cols", 3)
+    mean_abs = magnitude / (span * row_count * lax.axis_size("cols"))
+    return state[:, :span] / (mean_abs + 1e-06)
+
+
 def solution(mesh):
+    small = mesh.shape["cols"] == 4 and mesh.shape["rows"] % 2 == 0 and mesh.shape["rows"] <= 8
     return jax.shard_map(
-        body,
+        planes if small else general,
         mesh=mesh,
         in_specs=(P(("rows", "cols"), None), P(None, ("rows", "cols")), P(("rows", "cols"))),
         out_specs=P(None, ("rows", "cols")),

time: 178 us -> 49.9 us (0.28)
  blocking collectives: 170 us -> 0 us
  waiting for transfers between devices: 0 us -> 25.3 us
  starting transfers between devices: 0 us -> 12.4 us
  matrix products: 3.57 us -> 6.96 us
  other arithmetic: 2.03 us -> 3.87 us
    all_gather x6 -> x0, blocking collectives: 123 us -> none  [the longest x3 78.3 us: body(): v_piece = lax.all_gather(sending, 'rows', axis=0, tiled=True)]
    psum x4 -> x0, blocking collectives: 47.5 us -> none  [the longest x3 30.4 us: body(): summed = lax.psum(partial_value, 'cols')]
    ppermute x0 -> x13, waiting for transfers between devices: none -> 25.3 us  [swap(): lax.ppermute(value, axis, [(place, place ^ bit) for place in range(count)])]
    ppermute x0 -> x13, starting transfers between devices: none -> 12.4 us  [swap(): lax.ppermute(value, axis, [(place, place ^ bit) for place in range(count)])]
    dot_general x6 -> x4, matrix products: 3.57 us -> 6.96 us  [the longest x1 4.47 us: planes(): lax.dot_general(row_x, col_x, (((1,), (1,)), ((), ())), preferred_element...]
  transfers between devices with their start and end apart: 0 -> 13, of which waited for: 0 -> 10; matrix products, arithmetic and copies ran while one was open for 0% -> 2% of each run, Pallas kernels for 0% -> 0%
where the time goes in v1:
time: 49.9 us; the launch traced here: 49.7 us
  waiting for transfers between devices  25.3 us (51%)
  starting transfers between devices  12.4 us (25%)
  matrix products  6.96 us (14%)
  other arithmetic  3.87 us (8%)
  local copies, waits for them, and re-layouts  0.99 us (2%)
    ppermute x13, waiting for transfers between devices, swap(): lax.ppermute(value, axis, [(place, place ^ bit) for place in range(count)])  25.3 us
    ppermute x13, starting transfers between devices, swap(): lax.ppermute(value, axis, [(place, place ^ bit) for place in range(count)])  12.4 us
    dot_general x1, matrix products, planes(): lax.dot_general(row_x, col_x, (((1,), (1,)), ((), ())), preferred_element...  4.47 us
    dot_general x2, matrix products, to_cols(): lax.dot_general(v, kernel, (((1,), (0,)), ((), ())), preferred_element_ty...  1.3 us
    dot_general x1, matrix products, to_rows(): lax.dot_general(v, kernel, (((1,), (1,)), ((), ())), preferred_element_ty...  1.18 us
  transfers between devices with their start and end apart: 13, of which 10 were waited for; matrix products, arithmetic and copies ran while one was open for 2% of the time, Pallas kernels for 0%

profile of v1, /device:TPU:0, one launch (start us, length us, event | category | flops | bytes accessed | tf_op | source)
XLA Modules:
  0.0 49.7 jit_solution(16810311108494002260)
XLA Ops:
  0.0 0.7 %convert_element_type.42 = bf16[8,128]{1,0:T(8,128)(2,1)S(1)} convert(f32[8,128]{1,0:T(8,128)} %param.4) | non-fusion elementwise | flops 1024 | bytes 6144 | tf_op jit(solution)/shard_map/convert_element_type | solution.py:84
  0.7 0.7 %broadcast_in_dim.7 = bf16[8,128]{1,0:T(8,128)(2,1)S(1)} broadcast(bf16[128]{0:T(256)(128)(2,1)} %param.5), dimensions={1} | broadcast | bytes 2304 | tf_op jit(solution)/shard_map/broadcast_in_dim | solution.py:85
  1.3 0.8 %fusion.15 = (bf16[1,136,256]{2,1,0:T(8,128)(2,1)S(1)}, bf16[136,256]{1,0:T(8,128)(2,1)S(1)}) fusion(bf16[8,128]{1,0:T(8,128)(2,1)S(1)} %broadcast_in_dim.7, bf16[8,128]{1,0:T(8,128)(2,1)S(1)} %convert_element_type.42, bf16[128,256]{1,0:T(8,128)(2,1)} %param.3), kind=kLoop, calls=%fused_computation.42 | loop fusion | flops 208896 | bytes 208896 | tf_op jit(solution)/shard_map/stack | solution.py:91
  2.2 3.1 %collective-permute-start = (bf16[136,256]{1,0:T(8,128)(2,1)S(1)}, bf16[136,256]{1,0:T(8,128)(2,1)S(1)}, u32[]{:S(2)}, u32[]{:S(2)}) collective-permute-start(bf16[136,256]{1,0:T(8,128)(2,1)S(1)} %get-tuple-element.16), channel_id=1, source_target_pairs={{0,8},{4,12},{8,0},{12,4},{16,24},{20,28},{24,16},{28,20},{1,9},{5... | collective-permute-start | bytes 208904 | tf_op jit(solution)/shard_map/ppermute | solution.py:74
  5.3 2.6 %collective-permute-start.1 = (bf16[136,256]{1,0:T(8,128)(2,1)S(1)}, bf16[136,256]{1,0:T(8,128)(2,1)S(1)}, u32[]{:S(2)}, u32[]{:S(2)}) collective-permute-start(bf16[136,256]{1,0:T(8,128)(2,1)S(1)} %get-tuple-element.16), channel_id=1, source_target_pairs={{0,16},{4,20},{8,24},{12,28},{16,0},{20,4},{24,8},{28,12},{1,17},{... | collective-permute-start | bytes 208904 | tf_op jit(solution)/shard_map/ppermute | solution.py:74
  7.9 0.8 %constant_dynamic-update-slice_fusion.6 = (bf16[16,136,256]{2,1,0:T(8,128)(2,1)S(1)}, bf16[8,136,256]{2,1,0:T(8,128)(2,1)S(1)}) fusion(bf16[8,128]{1,0:T(8,128)(2,1)S(1)} %broadcast_in_dim.7, bf16[8,128]{1,0:T(8,128)(2,1)S(1)} %convert_element_type.42, bf16[128,256]{1,0:T(8,128)(2,1)} %param.3), kind=kLoop, calls=%fused_computation.27 | loop fusion | flops 208894 | bytes 208896
  8.8 4.1 %collective-permute-done.1 = bf16[136,256]{1,0:T(8,128)(2,1)S(1)} collective-permute-done((bf16[136,256]{1,0:T(8,128)(2,1)S(1)}, bf16[136,256]{1,0:T(8,128)(2,1)S(1)}, u32[]{:S(2)}, u32[]{:S(2)}) %collective-permute-start.1) | collective-permute-done | bytes 69664 | tf_op jit(solution)/shard_map/ppermute | solution.py:74
  12.8 1.3 %collective-permute-done.2 = bf16[136,256]{1,0:T(8,128)(2,1)S(1)} collective-permute-done((bf16[136,256]{1,0:T(8,128)(2,1)S(1)}, bf16[136,256]{1,0:T(8,128)(2,1)S(1)}, u32[]{:S(2)}, u32[]{:S(2)}) %collective-permute-start.2) | collective-permute-done | bytes 69664 | tf_op jit(solution)/shard_map/ppermute | solution.py:74
  14.2 1.6 %collective-permute-start.6 = (bf16[4,136,256]{2,1,0:T(8,128)(2,1)S(1)}, bf16[4,136,256]{2,1,0:T(8,128)(2,1)S(1)}, u32[]{:S(2)}, u32[]{:S(2)}) collective-permute-start(bf16[4,136,256]{2,1,0:T(8,128)(2,1)S(1)} %pad_maximum_fusion), channel_id=1, source_target_pairs={{0,4},{4,0},{8,12},{12,8},{16,20},{20,16},{24,28},{28,24},{1,5},{5... | collective-permute-start | bytes 835592 | tf_op jit(solution)/shard_map/ppermute | solution.py:74
  15.7 1.5 %collective-permute-start.3 = (bf16[4,136,256]{2,1,0:T(8,128)(2,1)S(1)}, bf16[4,136,256]{2,1,0:T(8,128)(2,1)S(1)}, u32[]{:S(2)}, u32[]{:S(2)}) collective-permute-start(bf16[4,136,256]{2,1,0:T(8,128)(2,1)S(1)} %pad_maximum_fusion), channel_id=1, source_target_pairs={{0,2},{1,3},{2,0},{3,1},{4,6},{5,7},{6,4},{7,5},{8,10},{9,11},{10,... | collective-permute-start | bytes 835592 | tf_op jit(solution)/shard_map/ppermute | solution.py:74
  17.3 5.0 %collective-permute-done.3 = bf16[4,136,256]{2,1,0:T(8,128)(2,1)S(1)} collective-permute-done((bf16[4,136,256]{2,1,0:T(8,128)(2,1)S(1)}, bf16[4,136,256]{2,1,0:T(8,128)(2,1)S(1)}, u32[]{:S(2)}, u32[]{:S(2)}) %collective-permute-start.3) | collective-permute-done | bytes 278560 | tf_op jit(solution)/shard_map/ppermute | solution.py:74
  22.4 0.2 multiply_reduce_fusion.1
  22.6 1.2 %collective-permute-done.5 = bf16[4,136,256]{2,1,0:T(8,128)(2,1)S(1)} collective-permute-done((bf16[4,136,256]{2,1,0:T(8,128)(2,1)S(1)}, bf16[4,136,256]{2,1,0:T(8,128)(2,1)S(1)}, u32[]{:S(2)}, u32[]{:S(2)}) %collective-permute-start.5) | collective-permute-done | bytes 278560 | tf_op jit(solution)/shard_map/ppermute | solution.py:74
  23.9 0.1 slice.65
  24.0 0.3 multiply_reduce_fusion
  24.3 4.5 %select_convert_fusion = bf16[2048,1024]{1,0:T(8,128)(2,1)S(1)} fusion(bf16[2048,256]{1,0:T(8,128)(2,1)S(1)} %bitcast.29, bf16[1024,256]{1,0:T(8,128)(2,1)S(1)} %bitcast.30, f32[1024]{0:T(1024)S(1)} %bitcast.38, f32[2048]{0:T(1024)S(1)} %bitcast.37, pred[2048]{0:T(1024)(128)(4,1)S(1)} %iota_compare_fusion.1), kind=kOutput, calls=%fused_computation | convolution fusion | flops 1090519040 | bytes 5781504 | tf_op jit(solution)/shard_map/dot_general | solution.py:111
  28.8 0.7 %fusion.5 = f32[8,1024]{1,0:T(8,128)S(1)} fusion(bf16[2048,1024]{1,0:T(8,128)(2,1)S(1)} %select_convert_fusion, bf16[16,136,256]{2,1,0:T(8,128)(2,1)S(1)} %constant_dynamic-update-slice_fusion), kind=kOutput, calls=%fused_computation.13 | convolution fusion | flops 33554432 | bytes 4259840 | tf_op jit(solution)/shard_map/dot_general | solution.py:124
  29.4 0.5 %collective-permute-start.7 = (f32[8,1024]{1,0:T(8,128)S(1)}, f32[8,1024]{1,0:T(8,128)S(1)}, u32[]{:S(2)}, u32[]{:S(2)}) collective-permute-start(f32[8,1024]{1,0:T(8,128)S(1)} %fusion.5), channel_id=1, source_target_pairs={{0,4},{4,0},{8,12},{12,8},{16,20},{20,16},{24,28},{28,24},{1,5},{5... | collective-permute-start | bytes 98312 | tf_op jit(solution)/shard_map/ppermute | solution.py:74
  30.0 3.4 %collective-permute-done.7 = f32[8,1024]{1,0:T(8,128)S(1)} collective-permute-done((f32[8,1024]{1,0:T(8,128)S(1)}, f32[8,1024]{1,0:T(8,128)S(1)}, u32[]{:S(2)}, u32[]{:S(2)}) %collective-permute-start.7) | collective-permute-done | bytes 32800 | tf_op jit(solution)/shard_map/ppermute | solution.py:74
  33.4 1.2 %fusion.10 = f32[8,2048]{1,0:T(8,128)S(1)} fusion(bf16[2048,1024]{1,0:T(8,128)(2,1)S(1)} %select_convert_fusion, f32[8,1024]{1,0:T(8,128)S(1)} %fusion.5, f32[8,512]{1,0:T(8,128)S(1)} %get-tuple-element.26, f32[8,512]{1,0:T(8,128)S(1)} %get-tuple-element.25, f32[1024]{0:T(1024)S(1)} %bitcast.34), kind=kOutput, calls=%fused_computation.33 | convolution fusion | flops 33587200 | bytes 4329472 | tf_op jit(solution)/shard_map/dot_general | solution.py:132
  34.6 1.3 %collective-permute-done.8 = f32[8,2048]{1,0:T(8,128)S(1)} collective-permute-done((f32[8,2048]{1,0:T(8,128)S(1)}, f32[8,2048]{1,0:T(8,128)S(1)}, u32[]{:S(2)}, u32[]{:S(2)}) %collective-permute-start.8) | collective-permute-done | bytes 65568 | tf_op jit(solution)/shard_map/ppermute | solution.py:74
  35.8 1.3 %collective-permute-start.9 = (f32[8,2048]{1,0:T(8,128)S(1)}, f32[8,2048]{1,0:T(8,128)S(1)}, u32[]{:S(2)}, u32[]{:S(2)}) collective-permute-start(f32[8,2048]{1,0:T(8,128)S(1)} %maximum_add_fusion), channel_id=1, source_target_pairs={{0,3},{1,2},{2,1},{3,0},{4,7},{5,6},{6,5},{7,4},{8,11},{9,10},{10,... | collective-permute-start | bytes 196616 | tf_op jit(solution)/shard_map/ppermute | solution.py:74
  37.2 2.8 %collective-permute-done.9 = f32[8,2048]{1,0:T(8,128)S(1)} collective-permute-done((f32[8,2048]{1,0:T(8,128)S(1)}, f32[8,2048]{1,0:T(8,128)S(1)}, u32[]{:S(2)}, u32[]{:S(2)}) %collective-permute-start.9) | collective-permute-done | bytes 65568 | tf_op jit(solution)/shard_map/ppermute | solution.py:74
  40.0 0.7 %fusion.3 = f32[8,1024]{1,0:T(8,128)S(1)} fusion(bf16[2048,1024]{1,0:T(8,128)(2,1)S(1)} %select_convert_fusion, f32[8,2048]{1,0:T(8,128)S(1)} %maximum_add_fusion, f32[8,512]{1,0:T(8,128)S(1)} %get-tuple-element.18, f32[8,512]{1,0:T(8,128)S(1)} %get-tuple-element.19, f32[8,512]{1,0:T(8,128)S(1)} %get-tuple-element.20, f32[8,512]{1,0:T(8,128)S(1)} %get-tuple-element.17, ...), kind=kOutput, calls=%fused_computation.11 | convolution fusion | flops 33652736 | bytes 4366336 | tf_op jit(solution)/shard_map/dot_general | solution.py:124
  40.6 0.5 %collective-permute-start.10 = (f32[8,1024]{1,0:T(8,128)S(1)}, f32[8,1024]{1,0:T(8,128)S(1)}, u32[]{:S(2)}, u32[]{:S(2)}) collective-permute-start(f32[8,1024]{1,0:T(8,128)S(1)} %fusion.3), channel_id=1, source_target_pairs={{0,4},{4,0},{8,12},{12,8},{16,20},{20,16},{24,28},{28,24},{1,5},{5... | collective-permute-start | bytes 98312 | tf_op jit(solution)/shard_map/ppermute | solution.py:74
  41.1 3.4 %collective-permute-done.10 = f32[8,1024]{1,0:T(8,128)S(1)} collective-permute-done((f32[8,1024]{1,0:T(8,128)S(1)}, f32[8,1024]{1,0:T(8,128)S(1)}, u32[]{:S(2)}, u32[]{:S(2)}) %collective-permute-start.10) | collective-permute-done | bytes 32800 | tf_op jit(solution)/shard_map/ppermute | solution.py:74
  44.5 0.1 abs_reduce_fusion
  44.7 0.1 broadcast_in_dim.9
  44.8 1.2 %collective-permute-done.11 = f32[8,128]{1,0:T(8,128)S(1)} collective-permute-done((f32[8,128]{1,0:T(8,128)S(1)}, f32[8,128]{1,0:T(8,128)S(1)}, u32[]{:S(2)}, u32[]{:S(2)}) %collective-permute-start.11) | collective-permute-done | bytes 4128 | tf_op jit(solution)/shard_map/ppermute | solution.py:74
  46.0 1.3 %collective-permute-start.12 = (f32[8,128]{1,0:T(8,128)S(1)}, f32[8,128]{1,0:T(8,128)S(1)}, u32[]{:S(2)}, u32[]{:S(2)}) collective-permute-start(f32[8,128]{1,0:T(8,128)S(1)} %broadcast_add_fusion), channel_id=1, source_target_pairs={{0,3},{1,2},{2,1},{3,0},{4,7},{5,6},{6,5},{7,4},{8,11},{9,10},{10,... | collective-permute-start | bytes 12296 | tf_op jit(solution)/shard_map/ppermute | solution.py:74
  47.3 1.8 %collective-permute-done.12 = f32[8,128]{1,0:T(8,128)S(1)} collective-permute-done((f32[8,128]{1,0:T(8,128)S(1)}, f32[8,128]{1,0:T(8,128)S(1)}, u32[]{:S(2)}, u32[]{:S(2)}) %collective-permute-start.12) | collective-permute-done | bytes 4128 | tf_op jit(solution)/shard_map/ppermute | solution.py:74
  49.0 0.7 %slice_divide_fusion = f32[8,128]{1,0:T(8,128)} fusion(f32[8,1024]{1,0:T(8,128)S(1)} %get-tuple-element.6, f32[8,128]{1,0:T(8,128)S(1)} %collective-permute-done.12, f32[8,128]{1,0:T(8,128)S(1)} %collective-permute-done.11, f32[8]{0:T(128)S(1)} %get-tuple-element.5), kind=kLoop, calls=%fused_computation.37 | loop fusion | flops 5120 | bytes 16416 | tf_op jit(solution)/shard_map/div | solution.py:151
  (26 shorter events, 0.3 us)
Async XLA Ops:
  2.2 6.6 %collective-permute-start = (bf16[136,256]{1,0:T(8,128)(2,1)S(1)}, bf16[136,256]{1,0:T(8,128)(2,1)S(1)}, u32[]{:S(2)}, u32[]{:S(2)}) collective-permute-start(bf16[136,256]{1,0:T(8,128)(2,1)S(1)} %get-tuple-element.16), channel_id=1, source_target_pairs={{0,8},{4,12},{8,0},{12,4},{16,24},{20,28},{24,16},{28,20},{1,9},{5... | collective-permute-start | bytes 208904 | tf_op jit(solution)/shard_map/ppermute | solution.py:74
  5.3 7.5 %collective-permute-start.1 = (bf16[136,256]{1,0:T(8,128)(2,1)S(1)}, bf16[136,256]{1,0:T(8,128)(2,1)S(1)}, u32[]{:S(2)}, u32[]{:S(2)}) collective-permute-start(bf16[136,256]{1,0:T(8,128)(2,1)S(1)} %get-tuple-element.16), channel_id=1, source_target_pairs={{0,16},{4,20},{8,24},{12,28},{16,0},{20,4},{24,8},{28,12},{1,17},{... | collective-permute-start | bytes 208904 | tf_op jit(solution)/shard_map/ppermute | solution.py:74
  7.9 6.2 %collective-permute-start.2 = (bf16[136,256]{1,0:T(8,128)(2,1)S(1)}, bf16[136,256]{1,0:T(8,128)(2,1)S(1)}, u32[]{:S(2)}, u32[]{:S(2)}) collective-permute-start(bf16[136,256]{1,0:T(8,128)(2,1)S(1)} %get-tuple-element.16), channel_id=1, source_target_pairs={{0,24},{4,28},{8,16},{12,20},{16,8},{20,12},{24,0},{28,4},{1,25},{... | collective-permute-start | bytes 208904 | tf_op jit(solution)/shard_map/ppermute | solution.py:74
  14.2 8.2 %collective-permute-start.6 = (bf16[4,136,256]{2,1,0:T(8,128)(2,1)S(1)}, bf16[4,136,256]{2,1,0:T(8,128)(2,1)S(1)}, u32[]{:S(2)}, u32[]{:S(2)}) collective-permute-start(bf16[4,136,256]{2,1,0:T(8,128)(2,1)S(1)} %pad_maximum_fusion), channel_id=1, source_target_pairs={{0,4},{4,0},{8,12},{12,8},{16,20},{20,16},{24,28},{28,24},{1,5},{5... | collective-permute-start | bytes 835592 | tf_op jit(solution)/shard_map/ppermute | solution.py:74
  15.7 6.5 %collective-permute-start.3 = (bf16[4,136,256]{2,1,0:T(8,128)(2,1)S(1)}, bf16[4,136,256]{2,1,0:T(8,128)(2,1)S(1)}, u32[]{:S(2)}, u32[]{:S(2)}) collective-permute-start(bf16[4,136,256]{2,1,0:T(8,128)(2,1)S(1)} %pad_maximum_fusion), channel_id=1, source_target_pairs={{0,2},{1,3},{2,0},{3,1},{4,6},{5,7},{6,4},{7,5},{8,10},{9,11},{10,... | collective-permute-start | bytes 835592 | tf_op jit(solution)/shard_map/ppermute | solution.py:74
  17.2 5.2 %collective-permute-start.4 = (bf16[4,136,256]{2,1,0:T(8,128)(2,1)S(1)}, bf16[4,136,256]{2,1,0:T(8,128)(2,1)S(1)}, u32[]{:S(2)}, u32[]{:S(2)}) collective-permute-start(bf16[4,136,256]{2,1,0:T(8,128)(2,1)S(1)} %pad_maximum_fusion), channel_id=1, source_target_pairs={{0,1},{1,0},{2,3},{3,2},{4,5},{5,4},{6,7},{7,6},{8,9},{9,8},{10,11... | collective-permute-start | bytes 835592 | tf_op jit(solution)/shard_map/ppermute | solution.py:74
  22.3 1.6 %collective-permute-start.5 = (bf16[4,136,256]{2,1,0:T(8,128)(2,1)S(1)}, bf16[4,136,256]{2,1,0:T(8,128)(2,1)S(1)}, u32[]{:S(2)}, u32[]{:S(2)}) collective-permute-start(bf16[4,136,256]{2,1,0:T(8,128)(2,1)S(1)} %collective-permute-done.3), channel_id=1, source_target_pairs={{0,1},{1,0},{2,3},{3,2},{4,5},{5,4},{6,7},{7,6},{8,9},{9,8},{10,11... | collective-permute-start | bytes 835592 | tf_op jit(solution)/shard_map/ppermute | solution.py:74
  29.4 3.9 %collective-permute-start.7 = (f32[8,1024]{1,0:T(8,128)S(1)}, f32[8,1024]{1,0:T(8,128)S(1)}, u32[]{:S(2)}, u32[]{:S(2)}) collective-permute-start(f32[8,1024]{1,0:T(8,128)S(1)} %fusion.5), channel_id=1, source_target_pairs={{0,4},{4,0},{8,12},{12,8},{16,20},{20,16},{24,28},{28,24},{1,5},{5... | collective-permute-start | bytes 98312 | tf_op jit(solution)/shard_map/ppermute | solution.py:74
  34.6 1.3 %collective-permute-start.8 = (f32[8,2048]{1,0:T(8,128)S(1)}, f32[8,2048]{1,0:T(8,128)S(1)}, u32[]{:S(2)}, u32[]{:S(2)}) collective-permute-start(f32[8,2048]{1,0:T(8,128)S(1)} %fusion.10), channel_id=1, source_target_pairs={{0,1},{1,0},{2,3},{3,2},{4,5},{5,4},{6,7},{7,6},{8,9},{9,8},{10,11... | collective-permute-start | bytes 196616 | tf_op jit(solution)/shard_map/ppermute | solution.py:74
  35.8 4.1 %collective-permute-start.9 = (f32[8,2048]{1,0:T(8,128)S(1)}, f32[8,2048]{1,0:T(8,128)S(1)}, u32[]{:S(2)}, u32[]{:S(2)}) collective-permute-start(f32[8,2048]{1,0:T(8,128)S(1)} %maximum_add_fusion), channel_id=1, source_target_pairs={{0,3},{1,2},{2,1},{3,0},{4,7},{5,6},{6,5},{7,4},{8,11},{9,10},{10,... | collective-permute-start | bytes 196616 | tf_op jit(solution)/shard_map/ppermute | solution.py:74
  40.6 3.9 %collective-permute-start.10 = (f32[8,1024]{1,0:T(8,128)S(1)}, f32[8,1024]{1,0:T(8,128)S(1)}, u32[]{:S(2)}, u32[]{:S(2)}) collective-permute-start(f32[8,1024]{1,0:T(8,128)S(1)} %fusion.3), channel_id=1, source_target_pairs={{0,4},{4,0},{8,12},{12,8},{16,20},{20,16},{24,28},{28,24},{1,5},{5... | collective-permute-start | bytes 98312 | tf_op jit(solution)/shard_map/ppermute | solution.py:74
  44.8 1.2 %collective-permute-start.11 = (f32[8,128]{1,0:T(8,128)S(1)}, f32[8,128]{1,0:T(8,128)S(1)}, u32[]{:S(2)}, u32[]{:S(2)}) collective-permute-start(f32[8,128]{1,0:T(8,128)S(1)} %broadcast_in_dim.9), channel_id=1, source_target_pairs={{0,1},{1,0},{2,3},{3,2},{4,5},{5,4},{6,7},{7,6},{8,9},{9,8},{10,11... | collective-permute-start | bytes 12296 | tf_op jit(solution)/shard_map/ppermute | solution.py:74
  46.0 3.0 %collective-permute-start.12 = (f32[8,128]{1,0:T(8,128)S(1)}, f32[8,128]{1,0:T(8,128)S(1)}, u32[]{:S(2)}, u32[]{:S(2)}) collective-permute-start(f32[8,128]{1,0:T(8,128)S(1)} %broadcast_add_fusion), channel_id=1, source_target_pairs={{0,3},{1,2},{2,1},{3,0},{4,7},{5,6},{6,5},{7,4},{8,11},{9,10},{10,... | collective-permute-start | bytes 12296 | tf_op jit(solution)/shard_map/ppermute | solution.py:74

commit v2 on v0

--- a/solution.py
+++ b/solution.py
@@ -1,12 +1,17 @@
+import functools
+import math
+
 import jax
 import jax.numpy as jnp
 from jax import lax
+from jax.experimental import pallas as pl
+from jax.experimental.pallas import tpu as pltpu
 from jax.sharding import PartitionSpec as P
 
 ITERS = 3
 
 
-def body(points, start_vectors, degree):
+def general(points, start_vectors, degree):
     row_count = lax.axis_size("rows")
     col_count = lax.axis_size("cols")
     row_place = lax.axis_index("rows")
@@ -24,6 +29,7 @@
     row_global = (
         row_place * col_count + row_slots // span_size
     ) * span_size + row_slots % span_size
+    x_piece = lax.all_gather(points, "rows", axis=0, tiled=True)
 
     def kernel_block(x_block, col_norms, first_slot):
         inner = lax.dot_general(
@@ -43,10 +49,9 @@
     for iteration in range(ITERS):
         empty = jnp.zeros((vectors.shape[0], row_total), jnp.float32)
         sending = vectors.T.astype(jnp.bfloat16)
-        x_piece = lax.all_gather(points, "rows", axis=0, tiled=True)
         v_piece = lax.all_gather(sending, "rows", axis=0, tiled=True)
         piece_rows = x_piece.shape[0]
-        block_size = 512
+        block_size = span_size * min(4, row_count)
         block_count = piece_rows // block_size
 
         def accumulate(block_index, running):
@@ -69,9 +74,241 @@
     return vectors / (mean_abs[:, None] + 1e-06)
 
 
+def swap(value, axis, bit):
+    count = lax.axis_size(axis)
+    return lax.ppermute(value, axis, [(place, place ^ bit) for place in range(count)])
+
+
+def call(body, outs, args, flops):
+    moved = sum(a.size * a.dtype.itemsize for a in args)
+    return pl.pallas_call(
+        body,
+        out_shape=outs,
+        in_specs=[pl.BlockSpec(memory_space=pltpu.VMEM)] * len(args),
+        out_specs=jax.tree.map(lambda _: pl.BlockSpec(memory_space=pltpu.VMEM), outs),
+        compiler_params=pltpu.CompilerParams(vmem_limit_bytes=16 * 2**20),
+        cost_estimate=pl.CostEstimate(flops=flops, bytes_accessed=moved, transcendentals=0),
+    )(*args)
+
+
+def dot(left, right, left_dim, right_dim):
+    return lax.dot_general(
+        left,
+        right,
+        (((left_dim,), (right_dim,)), ((), ())),
+        preferred_element_type=jnp.float32,
+    )
+
+
+def pack(scale, p_ref, v_ref, d_ref, out_ref):
+    span = p_ref.shape[0]
+    count = v_ref.shape[0]
+    x = p_ref[...]
+    f = x.astype(jnp.float32)
+    squares = f * f
+    high = squares.astype(jnp.bfloat16)
+    low = (squares - high.astype(jnp.float32)).astype(jnp.bfloat16)
+    ones = jnp.ones((count, x.shape[1]), jnp.bfloat16)
+    norm = (dot(ones, high, 1, 1) + dot(ones, low, 1, 1)) * scale
+    first = norm.astype(jnp.bfloat16).astype(jnp.float32)
+    second = (norm - first).astype(jnp.bfloat16).astype(jnp.float32)
+    third = norm - first - second
+    place = lax.broadcasted_iota(jnp.int32, norm.shape, 0)
+    degree = jnp.broadcast_to(d_ref[...].astype(jnp.float32), norm.shape)
+    side = jnp.where(place == 0, degree, jnp.where(place == 1, first, jnp.where(place == 2, second, third)))
+    out_ref[:span, :] = x
+    out_ref[span:, :span] = v_ref[...].astype(jnp.bfloat16)
+    out_ref[span:, span:] = side.astype(jnp.bfloat16)
+
+
+class Piece:
+    def __init__(self, ref, at):
+        self.ref, self.at = ref, at
+        self.span = ref.shape[1] - 8
+
+    def points(self):
+        return self.ref[self.at, : self.span, :]
+
+    def vectors(self):
+        return self.ref[self.at, self.span :, : self.span]
+
+    def side(self):
+        return self.ref[self.at, self.span :, self.span :].astype(jnp.float32)
+
+    def norm(self):
+        side = self.side()
+        return side[1:2] + side[2:3] + side[3:4]
+
+    def degree(self):
+        return self.side()[0:1]
+
+
+def pieces(refs):
+    return [Piece(ref, at) for ref in refs for at in range(ref.shape[0])]
+
+
+def wide(parts):
+    return jnp.concatenate(parts, axis=1)
+
+
+def fill(scale, rows, cols, out_ref, same=0):
+    span = rows[0].span
+    step = 2
+    for j in range(0, len(cols), step):
+        group = cols[j : j + step]
+        x = jnp.concatenate([c.points() for c in group], axis=0)
+        bias = wide([c.norm() for c in group])
+        for i, row in enumerate(rows):
+            tall = jnp.transpose(jnp.broadcast_to(row.norm(), (8, span)))[:, :1]
+            inner = dot(row.points(), x, 1, 1)
+            value = jnp.exp2(inner * (2.0 * scale) - bias - tall)
+            for k in range(len(group)):
+                if i == j + k < same:
+                    r = lax.broadcasted_iota(jnp.int32, value.shape, 0)
+                    c = lax.broadcasted_iota(jnp.int32, value.shape, 1)
+                    value = jnp.where(c == r + k * span, 0.0, value)
+            out_ref[i * span : (i + 1) * span, j * span : (j + len(group)) * span] = value.astype(
+                jnp.bfloat16
+            )
+
+
+def early(scale, sa, sb, ka, kb, xa, xka, ya, out_ref, part_ref):
+    rows = pieces([sa, sb, ka, kb, xa, xka])
+    cols = pieces([sa, sb, ya])
+    fill(scale, rows, cols, out_ref, sa.shape[0] + sb.shape[0])
+    part_ref[...] = dot(wide([r.vectors() for r in rows]), out_ref[...], 1, 0)
+
+
+def middle(scale, sa, sb, ka, kb, xa, xka, ya, xb, yb, part1, out_y, out_x, part_ref):
+    rows = pieces([sa, sb, ka, kb, xa, xka])
+    late = pieces([xb])
+    fill(scale, rows, pieces([yb]), out_y)
+    fill(scale, late, pieces([sa, sb, ya, yb]), out_x)
+    split = part1.shape[1]
+    part = dot(wide([r.vectors() for r in late]), out_x[...], 1, 0)
+    part_ref[:, :split] = part1[...] + part[:, :split]
+    part_ref[:, split:] = dot(wide([r.vectors() for r in rows]), out_y[...], 1, 0) + part[:, split:]
+
+
+def last(scale, sa, sb, ya, yb, xkb, part2, out_k, part_ref):
+    late = pieces([xkb])
+    fill(scale, late, pieces([sa, sb, ya, yb]), out_k)
+    part_ref[...] = part2[...] + dot(wide([r.vectors() for r in late]), out_k[...], 1, 0)
+
+
+def order(value, places, size):
+    return wide([value[:, p * size : (p + 1) * size] for p in places])
+
+
+def to_rows(sa, sb, ya, yb, a1, ay, ax, ak, part, other, out_ref):
+    degree = wide([c.degree() for c in pieces([sa, sb, ya, yb])])
+    block = degree.shape[1] // 4
+    state = (part[...] + order(other[...], (2, 3, 0, 1), block)) / degree
+    v = state.astype(jnp.bfloat16)
+    split = a1.shape[1]
+    r1 = a1.shape[0]
+    r2 = r1 + ax.shape[0]
+    out_ref[:, :r1] = dot(v[:, :split], a1[...], 1, 1) + dot(v[:, split:], ay[...], 1, 1)
+    out_ref[:, r1:r2] = dot(v, ax[...], 1, 1)
+    out_ref[:, r2:] = dot(v, ak[...], 1, 1)
+
+
+def to_cols(sa, sb, ka, kb, xa, xka, xb, xkb, a1, ay, ax, ak, part, other, out_ref):
+    degree = wide([c.degree() for c in pieces([sa, sb, ka, kb, xa, xka, xb, xkb])])
+    block = degree.shape[1] // 8
+    state = (part[...] + order(other[...], (5, 7, 4, 6, 2, 0, 3, 1), block)) / degree
+    v = state.astype(jnp.bfloat16)
+    split = a1.shape[1]
+    r1 = a1.shape[0]
+    r2 = r1 + ax.shape[0]
+    tail = dot(v[:, r1:r2], ax[...], 1, 0) + dot(v[:, r2:], ak[...], 1, 0)
+    out_ref[:, :split] = dot(v[:, :r1], a1[...], 1, 0) + tail[:, :split]
+    out_ref[:, split:] = dot(v[:, :r1], ay[...], 1, 0) + tail[:, split:]
+
+
+def finish(sa, sb, ya, yb, part, other, own_ref, sum_ref):
+    degree = wide([c.degree() for c in pieces([sa, sb, ya, yb])])
+    block = degree.shape[1] // 4
+    state = (part[...] + order(other[...], (2, 3, 0, 1), block)) / degree
+    own_ref[...] = state[:, : own_ref.shape[1]]
+    total = jnp.sum(jnp.abs(state), axis=1, keepdims=True)
+    sum_ref[...] = jnp.broadcast_to(total, sum_ref.shape)
+
+
+def planes(points, start_vectors, degree):
+    row_count = lax.axis_size("rows")
+    span, features = points.shape
+    count = start_vectors.shape[0]
+    scale = 4.0 / features * math.log2(math.e)
+
+    def shape(rows, cols, kind=jnp.float32):
+        return jax.ShapeDtypeStruct((rows, cols), kind)
+
+    message = call(
+        functools.partial(pack, scale),
+        shape(span + 8, features, jnp.bfloat16),
+        (points, start_vectors, degree[None, :]),
+        10**6,
+    )
+    remote = [swap(message, "rows", bit) for bit in range(2, row_count, 2)]
+    sa = jnp.stack([message, remote[0]])
+    sb = jnp.stack(remote[1:])
+    xa, ya, ka = swap(sa, "cols", 2), swap(sa, "rows", 1), swap(sa, "cols", 1)
+    xb, yb, kb = swap(sb, "cols", 2), swap(sb, "rows", 1), swap(sb, "cols", 1)
+    xka, xkb = swap(xa, "cols", 1), swap(xb, "cols", 1)
+
+    half = sa.shape[0] * span
+    rest = sb.shape[0] * span
+    r1 = 4 * half + 2 * rest
+    split = 2 * half + rest
+    width = split + rest
+    a1, part1 = call(
+        functools.partial(early, scale),
+        (shape(r1, split, jnp.bfloat16), shape(count, split)),
+        (sa, sb, ka, kb, xa, xka, ya),
+        2 * features * r1 * split,
+    )
+    ay, ax, part2 = call(
+        functools.partial(middle, scale),
+        (shape(r1, rest, jnp.bfloat16), shape(rest, width, jnp.bfloat16), shape(count, width)),
+        (sa, sb, ka, kb, xa, xka, ya, xb, yb, part1),
+        2 * features * (r1 * rest + rest * width),
+    )
+    ak, part = call(
+        functools.partial(last, scale),
+        (shape(rest, width, jnp.bfloat16), shape(count, width)),
+        (sa, sb, ya, yb, xkb, part2),
+        2 * features * rest * width,
+    )
+    part = call(
+        to_rows,
+        shape(count, r1 + 2 * rest),
+        (sa, sb, ya, yb, a1, ay, ax, ak, part, swap(part, "rows", 1)),
+        10**8,
+    )
+    part = part + order(swap(part, "cols", 1), (2, 3, 0, 1, 5, 4, 7, 6), rest)
+    part = call(
+        to_cols,
+        shape(count, width),
+        (sa, sb, ka, kb, xa, xka, xb, xkb, a1, ay, ax, ak, part, swap(part, "cols", 3)),
+        10**8,
+    )
+    own, total = call(
+        finish,
+        (shape(count, span), shape(count, span)),
+        (sa, sb, ya, yb, part, swap(part, "rows", 1)),
+        10**6,
+    )
+    total = total + swap(total, "cols", 1)
+    total = total + swap(total, "cols", 3)
+    mean_abs = total / (span * row_count * lax.axis_size("cols"))
+    return own / (mean_abs + 1e-06)
+
+
 def solution(mesh):
+    small = mesh.shape["cols"] == 4 and mesh.shape["rows"] == 8
     return jax.shard_map(
-        body,
+        planes if small else general,
         mesh=mesh,
         in_specs=(P(("rows", "cols"), None), P(None, ("rows", "cols")), P(("rows", "cols"))),
         out_specs=P(None, ("rows", "cols")),

time: 178 us -> 46.9 us (0.26)
  blocking collectives: 170 us -> 0 us
  waiting for transfers between devices: 0 us -> 21 us
  starting transfers between devices: 0 us -> 16.3 us
  Pallas kernels: 0 us -> 6.45 us
  matrix products: 3.57 us -> 0 us
    all_gather x6 -> x0, blocking collectives: 123 us -> none  [the longest x3 78.3 us: body(): v_piece = lax.all_gather(sending, 'rows', axis=0, tiled=True)]
    psum x4 -> x0, blocking collectives: 47.5 us -> none  [the longest x3 30.4 us: body(): summed = lax.psum(partial_value, 'cols')]
    ppermute x0 -> x17, waiting for transfers between devices: none -> 21 us  [swap(): lax.ppermute(value, axis, [(place, place ^ bit) for place in range(count)])]
    ppermute x0 -> x17, starting transfers between devices: none -> 16.3 us  [swap(): lax.ppermute(value, axis, [(place, place ^ bit) for place in range(count)])]
    pallas_call x0 -> x7, Pallas kernels: none -> 6.45 us  [call(): pl.pallas_call(body, out_shape=outs, in_specs=[pl.BlockSpec(memory_space=...]
    dot_general x6 -> x0, matrix products: 3.57 us -> none  [accumulate(): lax.dot_general(v_block, kernel, (((0,), (1,)), ((), ())), preferred_elem...]
  transfers between devices with their start and end apart: 0 -> 17, of which waited for: 0 -> 11; matrix products, arithmetic and copies ran while one was open for 0% -> 0% of each run, Pallas kernels for 0% -> 8%
where the time goes in v2:
time: 46.9 us; the launch traced here: 46.7 us
  waiting for transfers between devices  21 us (45%)
  starting transfers between devices  16.3 us (35%)
  Pallas kernels  6.45 us (14%)
  local copies, waits for them, and re-layouts  2.19 us (5%)
  other arithmetic  0.65 us (1%)
    ppermute x17, waiting for transfers between devices, swap(): lax.ppermute(value, axis, [(place, place ^ bit) for place in range(count)])  21 us
    ppermute x17, starting transfers between devices, swap(): lax.ppermute(value, axis, [(place, place ^ bit) for place in range(count)])  16.3 us
    pallas_call x7, Pallas kernels, call(): pl.pallas_call(body, out_shape=outs, in_specs=[pl.BlockSpec(memory_space=...  6.45 us
    unnamed x11, local copies, waits for them, and re-layouts  2.19 us
  transfers between devices with their start and end apart: 17, of which 11 were waited for; matrix products, arithmetic and copies ran while one was open for 0% of the time, Pallas kernels for 8%

profile of v2, /device:TPU:0, one launch (start us, length us, event | category | flops | bytes accessed | tf_op | source)
XLA Modules:
  0.0 46.7 jit_solution(11256983916892816963)
XLA Ops:
  0.0 0.8 %copy-done = bf16[128,256]{1,0:T(8,128)(2,1)S(1)} copy-done((bf16[128,256]{1,0:T(8,128)(2,1)S(1)}, bf16[128,256]{1,0:T(8,128)(2,1)}, u32[]{:S(2)}) %copy-start) | copy-done | bytes 65560
  0.8 0.7 %copy-done.1 = f32[8,128]{1,0:T(8,128)S(1)} copy-done((f32[8,128]{1,0:T(8,128)S(1)}, f32[8,128]{1,0:T(8,128)}, u32[]{:S(2)}) %copy-start.1) | copy-done | bytes 4120
  1.5 0.7 %copy-done.2 = bf16[128]{0:T(256)(128)(2,1)S(1)} copy-done((bf16[128]{0:T(256)(128)(2,1)S(1)}, bf16[128]{0:T(256)(128)(2,1)}, u32[]{:S(2)}) %copy-start.2) | copy-done | bytes 280
  2.2 0.2 shard_map.37
  2.3 3.1 %collective-permute-start = (bf16[136,256]{1,0:T(8,128)(2,1)S(1)}, bf16[136,256]{1,0:T(8,128)(2,1)S(1)}, u32[]{:S(2)}, u32[]{:S(2)}) collective-permute-start(bf16[136,256]{1,0:T(8,128)(2,1)S(1)} %shard_map.37), channel_id=1, source_target_pairs={{0,8},{4,12},{8,0},{12,4},{16,24},{20,28},{24,16},{28,20},{1,9},{5... | collective-permute-start | bytes 208904 | tf_op jit(solution)/shard_map/ppermute | solution.py:79
  5.5 2.5 %collective-permute-start.2 = (bf16[136,256]{1,0:T(8,128)(2,1)S(1)}, bf16[136,256]{1,0:T(8,128)(2,1)S(1)}, u32[]{:S(2)}, u32[]{:S(2)}) collective-permute-start(bf16[136,256]{1,0:T(8,128)(2,1)S(1)} %shard_map.37), channel_id=1, source_target_pairs={{0,24},{4,28},{8,16},{12,20},{16,8},{20,12},{24,0},{28,4},{1,25},{... | collective-permute-start | bytes 208904 | tf_op jit(solution)/shard_map/ppermute | solution.py:79
  8.1 1.7 %collective-permute-start.7 = (bf16[2,136,256]{2,1,0:T(8,128)(2,1)S(1)}, bf16[2,136,256]{2,1,0:T(8,128)(2,1)S(1)}, u32[]{:S(2)}, u32[]{:S(2)}) collective-permute-start(bf16[2,136,256]{2,1,0:T(8,128)(2,1)S(1)} %pad_maximum_fusion.sa), channel_id=1, source_target_pairs={{0,2},{1,3},{2,0},{3,1},{4,6},{5,7},{6,4},{7,5},{8,10},{9,11},{10,... | collective-permute-start | bytes 417800 | tf_op jit(solution)/shard_map/ppermute | solution.py:79
  9.8 2.7 %collective-permute-done.2 = bf16[136,256]{1,0:T(8,128)(2,1)S(1)} collective-permute-done((bf16[136,256]{1,0:T(8,128)(2,1)S(1)}, bf16[136,256]{1,0:T(8,128)(2,1)S(1)}, u32[]{:S(2)}, u32[]{:S(2)}) %collective-permute-start.2) | collective-permute-done | bytes 69664 | tf_op jit(solution)/shard_map/ppermute | solution.py:79
  12.5 2.2 %collective-permute-done.1 = bf16[136,256]{1,0:T(8,128)(2,1)S(1)} collective-permute-done((bf16[136,256]{1,0:T(8,128)(2,1)S(1)}, bf16[136,256]{1,0:T(8,128)(2,1)S(1)}, u32[]{:S(2)}, u32[]{:S(2)}) %collective-permute-start.1) | collective-permute-done | bytes 69664 | tf_op jit(solution)/shard_map/ppermute | solution.py:79
  14.7 1.6 %collective-permute-start.9 = (bf16[2,136,256]{2,1,0:T(8,128)(2,1)S(1)}, bf16[2,136,256]{2,1,0:T(8,128)(2,1)S(1)}, u32[]{:S(2)}, u32[]{:S(2)}) collective-permute-start(bf16[2,136,256]{2,1,0:T(8,128)(2,1)S(1)} %pad_maximum_fusion.1.sb), channel_id=1, source_target_pairs={{0,2},{1,3},{2,0},{3,1},{4,6},{5,7},{6,4},{7,5},{8,10},{9,11},{10,... | collective-permute-start | bytes 417800 | tf_op jit(solution)/shard_map/ppermute | solution.py:79
  16.3 1.5 %collective-permute-start.3 = (bf16[2,136,256]{2,1,0:T(8,128)(2,1)S(1)}, bf16[2,136,256]{2,1,0:T(8,128)(2,1)S(1)}, u32[]{:S(2)}, u32[]{:S(2)}) collective-permute-start(bf16[2,136,256]{2,1,0:T(8,128)(2,1)S(1)} %pad_maximum_fusion.sa), channel_id=1, source_target_pairs={{0,4},{4,0},{8,12},{12,8},{16,20},{20,16},{24,28},{28,24},{1,5},{5... | collective-permute-start | bytes 417800 | tf_op jit(solution)/shard_map/ppermute | solution.py:79
  17.8 0.5 %collective-permute-start.8 = (bf16[2,136,256]{2,1,0:T(8,128)(2,1)S(1)}, bf16[2,136,256]{2,1,0:T(8,128)(2,1)S(1)}, u32[]{:S(2)}, u32[]{:S(2)}) collective-permute-start(bf16[2,136,256]{2,1,0:T(8,128)(2,1)S(1)} %collective-permute-done.7.xa), channel_id=1, source_target_pairs={{0,1},{1,0},{2,3},{3,2},{4,5},{5,4},{6,7},{7,6},{8,9},{9,8},{10,11... | collective-permute-start | bytes 417800 | tf_op jit(solution)/shard_map/ppermute | solution.py:79
  18.3 0.5 %collective-permute-start.4 = (bf16[2,136,256]{2,1,0:T(8,128)(2,1)S(1)}, bf16[2,136,256]{2,1,0:T(8,128)(2,1)S(1)}, u32[]{:S(2)}, u32[]{:S(2)}) collective-permute-start(bf16[2,136,256]{2,1,0:T(8,128)(2,1)S(1)} %pad_maximum_fusion.1.sb), channel_id=1, source_target_pairs={{0,4},{4,0},{8,12},{12,8},{16,20},{20,16},{24,28},{28,24},{1,5},{5... | collective-permute-start | bytes 417800 | tf_op jit(solution)/shard_map/ppermute | solution.py:79
  18.8 1.5 %collective-permute-done.9.xb = bf16[2,136,256]{2,1,0:T(8,128)(2,1)S(1)} collective-permute-done((bf16[2,136,256]{2,1,0:T(8,128)(2,1)S(1)}, bf16[2,136,256]{2,1,0:T(8,128)(2,1)S(1)}, u32[]{:S(2)}, u32[]{:S(2)}) %collective-permute-start.9) | collective-permute-done | bytes 139296 | tf_op jit(solution)/shard_map/ppermute | solution.py:79
  20.3 1.7 %collective-permute-done.3.ya = bf16[2,136,256]{2,1,0:T(8,128)(2,1)S(1)} collective-permute-done((bf16[2,136,256]{2,1,0:T(8,128)(2,1)S(1)}, bf16[2,136,256]{2,1,0:T(8,128)(2,1)S(1)}, u32[]{:S(2)}, u32[]{:S(2)}) %collective-permute-start.3) | collective-permute-done | bytes 139296 | tf_op jit(solution)/shard_map/ppermute | solution.py:79
  22.0 2.2 %shard_map.38 = (bf16[1536,768]{1,0:T(8,128)(2,1)S(1)}, f32[8,768]{1,0:T(8,128)S(1)}) custom-call(bf16[2,136,256]{2,1,0:T(8,128)(2,1)S(1)} %pad_maximum_fusion.sa, bf16[2,136,256]{2,1,0:T(8,128)(2,1)S(1)} %pad_maximum_fusion.1.sb, bf16[2,136,256]{2,1,0:T(8,128)(2,1)S(1)} %collective-permute-done.5.ka, bf16[2,136,256]{2,1,0:T(8,128)(2,1)S(1)} %collective-permute-done.6.kb, ...), custom_call_target="tpu_custom_call" | custom-call | flops 603979776 | bytes 974848 | tf_op jit(solution)/shard_map/pallas_call | solution.py:84
  24.2 0.2 collective-permute-done.4.yb
  24.5 1.5 %shard_map.39 = (bf16[1536,256]{1,0:T(8,128)(2,1)S(1)}, bf16[256,1024]{1,0:T(8,128)(2,1)S(1)}, f32[8,1024]{1,0:T(8,128)S(1)}) custom-call(bf16[2,136,256]{2,1,0:T(8,128)(2,1)S(1)} %pad_maximum_fusion.sa, bf16[2,136,256]{2,1,0:T(8,128)(2,1)S(1)} %pad_maximum_fusion.1.sb, bf16[2,136,256]{2,1,0:T(8,128)(2,1)S(1)} %collective-permute-done.5.ka, ...), custom_call_target="tpu_custom_call" | custom-call | flops 335544320 | bytes 1277952 | tf_op jit(solution)/shard_map/pallas_call | solution.py:84
  25.9 0.7 %shard_map.40 = (bf16[256,1024]{1,0:T(8,128)(2,1)S(1)}, f32[8,1024]{1,0:T(8,128)S(1)}) custom-call(bf16[2,136,256]{2,1,0:T(8,128)(2,1)S(1)} %pad_maximum_fusion.sa, bf16[2,136,256]{2,1,0:T(8,128)(2,1)S(1)} %pad_maximum_fusion.1.sb, bf16[2,136,256]{2,1,0:T(8,128)(2,1)S(1)} %collective-permute-done.3.ya, bf16[2,136,256]{2,1,0:T(8,128)(2,1)S(1)} %collective-permute-done.4.yb, ...), custom_call_target="tpu_custom_call" | custom-call | flops 134217728 | bytes 729088 | tf_op jit(solution)/shard_map/pallas_call | solution.py:84
  26.6 2.1 %collective-permute-start.11 = (f32[8,1024]{1,0:T(8,128)S(1)}, f32[8,1024]{1,0:T(8,128)S(1)}, u32[]{:S(2)}, u32[]{:S(2)}) collective-permute-start(f32[8,1024]{1,0:T(8,128)S(1)} %get-tuple-element.20.part), channel_id=1, source_target_pairs={{0,4},{4,0},{8,12},{12,8},{16,20},{20,16},{24,28},{28,24},{1,5},{5... | collective-permute-start | bytes 98312 | tf_op jit(solution)/shard_map/ppermute | solution.py:79
  28.7 1.9 %collective-permute-done.11.other = f32[8,1024]{1,0:T(8,128)S(1)} collective-permute-done((f32[8,1024]{1,0:T(8,128)S(1)}, f32[8,1024]{1,0:T(8,128)S(1)}, u32[]{:S(2)}, u32[]{:S(2)}) %collective-permute-start.11) | collective-permute-done | bytes 32800 | tf_op jit(solution)/shard_map/ppermute | solution.py:79
  30.6 1.2 %shard_map.41 = f32[8,2048]{1,0:T(8,128)S(1)} custom-call(bf16[2,136,256]{2,1,0:T(8,128)(2,1)S(1)} %pad_maximum_fusion.sa, bf16[2,136,256]{2,1,0:T(8,128)(2,1)S(1)} %pad_maximum_fusion.1.sb, bf16[2,136,256]{2,1,0:T(8,128)(2,1)S(1)} %collective-permute-done.3.ya, bf16[2,136,256]{2,1,0:T(8,128)(2,1)S(1)} %collective-permute-done.4.yb, ...), custom_call_target="tpu_custom_call" | custom-call | flops 100000000 | bytes 4816896 | tf_op jit(solution)/shard_map/pallas_call | solution.py:84
  31.8 1.3 %collective-permute-done.12 = f32[8,2048]{1,0:T(8,128)S(1)} collective-permute-done((f32[8,2048]{1,0:T(8,128)S(1)}, f32[8,2048]{1,0:T(8,128)S(1)}, u32[]{:S(2)}, u32[]{:S(2)}) %collective-permute-start.12) | collective-permute-done | bytes 65568 | tf_op jit(solution)/shard_map/ppermute | solution.py:79
  33.1 0.4 collective-permute-start.13
  33.5 3.8 %collective-permute-done.13.other = f32[8,2048]{1,0:T(8,128)S(1)} collective-permute-done((f32[8,2048]{1,0:T(8,128)S(1)}, f32[8,2048]{1,0:T(8,128)S(1)}, u32[]{:S(2)}, u32[]{:S(2)}) %collective-permute-start.13) | collective-permute-done | bytes 65568 | tf_op jit(solution)/shard_map/ppermute | solution.py:79
  37.3 0.6 %shard_map.42.part = f32[8,1024]{1,0:T(8,128)S(1)} custom-call(bf16[2,136,256]{2,1,0:T(8,128)(2,1)S(1)} %pad_maximum_fusion.sa, bf16[2,136,256]{2,1,0:T(8,128)(2,1)S(1)} %pad_maximum_fusion.1.sb, bf16[2,136,256]{2,1,0:T(8,128)(2,1)S(1)} %collective-permute-done.5.ka, bf16[2,136,256]{2,1,0:T(8,128)(2,1)S(1)} %collective-permute-done.6.kb, ...), custom_call_target="tpu_custom_call" | custom-call | flops 100000000 | bytes 5439488 | tf_op jit(solution)/shard_map/pallas_call | solution.py:84
  37.9 2.0 %collective-permute-start.14 = (f32[8,1024]{1,0:T(8,128)S(1)}, f32[8,1024]{1,0:T(8,128)S(1)}, u32[]{:S(2)}, u32[]{:S(2)}) collective-permute-start(f32[8,1024]{1,0:T(8,128)S(1)} %shard_map.42.part), channel_id=1, source_target_pairs={{0,4},{4,0},{8,12},{12,8},{16,20},{20,16},{24,28},{28,24},{1,5},{5... | collective-permute-start | bytes 98312 | tf_op jit(solution)/shard_map/ppermute | solution.py:79
  39.9 1.9 %collective-permute-done.14.other = f32[8,1024]{1,0:T(8,128)S(1)} collective-permute-done((f32[8,1024]{1,0:T(8,128)S(1)}, f32[8,1024]{1,0:T(8,128)S(1)}, u32[]{:S(2)}, u32[]{:S(2)}) %collective-permute-start.14) | collective-permute-done | bytes 32800 | tf_op jit(solution)/shard_map/ppermute | solution.py:79
  41.9 1.2 %collective-permute-done.15 = f32[8,128]{1,0:T(8,128)S(1)} collective-permute-done((f32[8,128]{1,0:T(8,128)S(1)}, f32[8,128]{1,0:T(8,128)S(1)}, u32[]{:S(2)}, u32[]{:S(2)}) %collective-permute-start.15) | collective-permute-done | bytes 4128 | tf_op jit(solution)/shard_map/ppermute | solution.py:79
  43.1 0.3 collective-permute-start.16
  43.4 2.7 %collective-permute-done.16 = f32[8,128]{1,0:T(8,128)S(1)} collective-permute-done((f32[8,128]{1,0:T(8,128)S(1)}, f32[8,128]{1,0:T(8,128)S(1)}, u32[]{:S(2)}, u32[]{:S(2)}) %collective-permute-start.16) | collective-permute-done | bytes 4128 | tf_op jit(solution)/shard_map/ppermute | solution.py:79
  46.1 0.6 %add_divide_fusion = f32[8,128]{1,0:T(8,128)} fusion(f32[8,128]{1,0:T(8,128)S(1)} %get-tuple-element.21, f32[8,128]{1,0:T(8,128)S(1)} %add.16, f32[8,128]{1,0:T(8,128)S(1)} %collective-permute-done.16), kind=kLoop, calls=%fused_computation.8 | loop fusion | flops 4096 | bytes 16384 | tf_op jit(solution)/shard_map/div | solution.py:305
  (26 shorter events, 0.3 us)
Async XLA Ops:
  0.0 0.8 %copy-start = (bf16[128,256]{1,0:T(8,128)(2,1)S(1)}, bf16[128,256]{1,0:T(8,128)(2,1)}, u32[]{:S(2)}) copy-start(bf16[128,256]{1,0:T(8,128)(2,1)} %p_ref.1) | copy-start | bytes 196612
  0.8 0.7 %copy-start.1 = (f32[8,128]{1,0:T(8,128)S(1)}, f32[8,128]{1,0:T(8,128)}, u32[]{:S(2)}) copy-start(f32[8,128]{1,0:T(8,128)} %v_ref.1) | copy-start | bytes 12292
  1.5 0.7 %copy-start.2 = (bf16[128]{0:T(256)(128)(2,1)S(1)}, bf16[128]{0:T(256)(128)(2,1)}, u32[]{:S(2)}) copy-start(bf16[128]{0:T(256)(128)(2,1)} %param.5) | copy-start | bytes 772
  2.3 5.7 %collective-permute-start = (bf16[136,256]{1,0:T(8,128)(2,1)S(1)}, bf16[136,256]{1,0:T(8,128)(2,1)S(1)}, u32[]{:S(2)}, u32[]{:S(2)}) collective-permute-start(bf16[136,256]{1,0:T(8,128)(2,1)S(1)} %shard_map.37), channel_id=1, source_target_pairs={{0,8},{4,12},{8,0},{12,4},{16,24},{20,28},{24,16},{28,20},{1,9},{5... | collective-permute-start | bytes 208904 | tf_op jit(solution)/shard_map/ppermute | solution.py:79
  5.5 7.0 %collective-permute-start.2 = (bf16[136,256]{1,0:T(8,128)(2,1)S(1)}, bf16[136,256]{1,0:T(8,128)(2,1)S(1)}, u32[]{:S(2)}, u32[]{:S(2)}) collective-permute-start(bf16[136,256]{1,0:T(8,128)(2,1)S(1)} %shard_map.37), channel_id=1, source_target_pairs={{0,24},{4,28},{8,16},{12,20},{16,8},{20,12},{24,0},{28,4},{1,25},{... | collective-permute-start | bytes 208904 | tf_op jit(solution)/shard_map/ppermute | solution.py:79
  7.9 6.8 %collective-permute-start.1 = (bf16[136,256]{1,0:T(8,128)(2,1)S(1)}, bf16[136,256]{1,0:T(8,128)(2,1)S(1)}, u32[]{:S(2)}, u32[]{:S(2)}) collective-permute-start(bf16[136,256]{1,0:T(8,128)(2,1)S(1)} %shard_map.37), channel_id=1, source_target_pairs={{0,16},{4,20},{8,24},{12,28},{16,0},{20,4},{24,8},{28,12},{1,17},{... | collective-permute-start | bytes 208904 | tf_op jit(solution)/shard_map/ppermute | solution.py:79
  8.1 9.7 %collective-permute-start.7 = (bf16[2,136,256]{2,1,0:T(8,128)(2,1)S(1)}, bf16[2,136,256]{2,1,0:T(8,128)(2,1)S(1)}, u32[]{:S(2)}, u32[]{:S(2)}) collective-permute-start(bf16[2,136,256]{2,1,0:T(8,128)(2,1)S(1)} %pad_maximum_fusion.sa), channel_id=1, source_target_pairs={{0,2},{1,3},{2,0},{3,1},{4,6},{5,7},{6,4},{7,5},{8,10},{9,11},{10,... | collective-permute-start | bytes 417800 | tf_op jit(solution)/shard_map/ppermute | solution.py:79
  9.8 8.5 %collective-permute-start.5 = (bf16[2,136,256]{2,1,0:T(8,128)(2,1)S(1)}, bf16[2,136,256]{2,1,0:T(8,128)(2,1)S(1)}, u32[]{:S(2)}, u32[]{:S(2)}) collective-permute-start(bf16[2,136,256]{2,1,0:T(8,128)(2,1)S(1)} %pad_maximum_fusion.sa), channel_id=1, source_target_pairs={{0,1},{1,0},{2,3},{3,2},{4,5},{5,4},{6,7},{7,6},{8,9},{9,8},{10,11... | collective-permute-start | bytes 417800 | tf_op jit(solution)/shard_map/ppermute | solution.py:79
  14.7 5.6 %collective-permute-start.9 = (bf16[2,136,256]{2,1,0:T(8,128)(2,1)S(1)}, bf16[2,136,256]{2,1,0:T(8,128)(2,1)S(1)}, u32[]{:S(2)}, u32[]{:S(2)}) collective-permute-start(bf16[2,136,256]{2,1,0:T(8,128)(2,1)S(1)} %pad_maximum_fusion.1.sb), channel_id=1, source_target_pairs={{0,2},{1,3},{2,0},{3,1},{4,6},{5,7},{6,4},{7,5},{8,10},{9,11},{10,... | collective-permute-start | bytes 417800 | tf_op jit(solution)/shard_map/ppermute | solution.py:79
  16.3 5.7 %collective-permute-start.3 = (bf16[2,136,256]{2,1,0:T(8,128)(2,1)S(1)}, bf16[2,136,256]{2,1,0:T(8,128)(2,1)S(1)}, u32[]{:S(2)}, u32[]{:S(2)}) collective-permute-start(bf16[2,136,256]{2,1,0:T(8,128)(2,1)S(1)} %pad_maximum_fusion.sa), channel_id=1, source_target_pairs={{0,4},{4,0},{8,12},{12,8},{16,20},{20,16},{24,28},{28,24},{1,5},{5... | collective-permute-start | bytes 417800 | tf_op jit(solution)/shard_map/ppermute | solution.py:79
  17.8 4.2 %collective-permute-start.6 = (bf16[2,136,256]{2,1,0:T(8,128)(2,1)S(1)}, bf16[2,136,256]{2,1,0:T(8,128)(2,1)S(1)}, u32[]{:S(2)}, u32[]{:S(2)}) collective-permute-start(bf16[2,136,256]{2,1,0:T(8,128)(2,1)S(1)} %pad_maximum_fusion.1.sb), channel_id=1, source_target_pairs={{0,1},{1,0},{2,3},{3,2},{4,5},{5,4},{6,7},{7,6},{8,9},{9,8},{10,11... | collective-permute-start | bytes 417800 | tf_op jit(solution)/shard_map/ppermute | solution.py:79
  17.8 4.2 %collective-permute-start.8 = (bf16[2,136,256]{2,1,0:T(8,128)(2,1)S(1)}, bf16[2,136,256]{2,1,0:T(8,128)(2,1)S(1)}, u32[]{:S(2)}, u32[]{:S(2)}) collective-permute-start(bf16[2,136,256]{2,1,0:T(8,128)(2,1)S(1)} %collective-permute-done.7.xa), channel_id=1, source_target_pairs={{0,1},{1,0},{2,3},{3,2},{4,5},{5,4},{6,7},{7,6},{8,9},{9,8},{10,11... | collective-permute-start | bytes 417800 | tf_op jit(solution)/shard_map/ppermute | solution.py:79
  18.3 6.2 %collective-permute-start.4 = (bf16[2,136,256]{2,1,0:T(8,128)(2,1)S(1)}, bf16[2,136,256]{2,1,0:T(8,128)(2,1)S(1)}, u32[]{:S(2)}, u32[]{:S(2)}) collective-permute-start(bf16[2,136,256]{2,1,0:T(8,128)(2,1)S(1)} %pad_maximum_fusion.1.sb), channel_id=1, source_target_pairs={{0,4},{4,0},{8,12},{12,8},{16,20},{20,16},{24,28},{28,24},{1,5},{5... | collective-permute-start | bytes 417800 | tf_op jit(solution)/shard_map/ppermute | solution.py:79
  20.3 5.7 %collective-permute-start.10 = (bf16[2,136,256]{2,1,0:T(8,128)(2,1)S(1)}, bf16[2,136,256]{2,1,0:T(8,128)(2,1)S(1)}, u32[]{:S(2)}, u32[]{:S(2)}) collective-permute-start(bf16[2,136,256]{2,1,0:T(8,128)(2,1)S(1)} %collective-permute-done.9.xb), channel_id=1, source_target_pairs={{0,1},{1,0},{2,3},{3,2},{4,5},{5,4},{6,7},{7,6},{8,9},{9,8},{10,11... | collective-permute-start | bytes 417800 | tf_op jit(solution)/shard_map/ppermute | solution.py:79
  26.6 4.0 %collective-permute-start.11 = (f32[8,1024]{1,0:T(8,128)S(1)}, f32[8,1024]{1,0:T(8,128)S(1)}, u32[]{:S(2)}, u32[]{:S(2)}) collective-permute-start(f32[8,1024]{1,0:T(8,128)S(1)} %get-tuple-element.20.part), channel_id=1, source_target_pairs={{0,4},{4,0},{8,12},{12,8},{16,20},{20,16},{24,28},{28,24},{1,5},{5... | collective-permute-start | bytes 98312 | tf_op jit(solution)/shard_map/ppermute | solution.py:79
  31.8 1.3 %collective-permute-start.12 = (f32[8,2048]{1,0:T(8,128)S(1)}, f32[8,2048]{1,0:T(8,128)S(1)}, u32[]{:S(2)}, u32[]{:S(2)}) collective-permute-start(f32[8,2048]{1,0:T(8,128)S(1)} %shard_map.41), channel_id=1, source_target_pairs={{0,1},{1,0},{2,3},{3,2},{4,5},{5,4},{6,7},{7,6},{8,9},{9,8},{10,11... | collective-permute-start | bytes 196616 | tf_op jit(solution)/shard_map/ppermute | solution.py:79
  33.1 4.1 %collective-permute-start.13 = (f32[8,2048]{1,0:T(8,128)S(1)}, f32[8,2048]{1,0:T(8,128)S(1)}, u32[]{:S(2)}, u32[]{:S(2)}) collective-permute-start(f32[8,2048]{1,0:T(8,128)S(1)} %add.15.part), channel_id=1, source_target_pairs={{0,3},{1,2},{2,1},{3,0},{4,7},{5,6},{6,5},{7,4},{8,11},{9,10},{10,... | collective-permute-start | bytes 196616 | tf_op jit(solution)/shard_map/ppermute | solution.py:79
  37.9 3.9 %collective-permute-start.14 = (f32[8,1024]{1,0:T(8,128)S(1)}, f32[8,1024]{1,0:T(8,128)S(1)}, u32[]{:S(2)}, u32[]{:S(2)}) collective-permute-start(f32[8,1024]{1,0:T(8,128)S(1)} %shard_map.42.part), channel_id=1, source_target_pairs={{0,4},{4,0},{8,12},{12,8},{16,20},{20,16},{24,28},{28,24},{1,5},{5... | collective-permute-start | bytes 98312 | tf_op jit(solution)/shard_map/ppermute | solution.py:79
  41.9 1.2 %collective-permute-start.15 = (f32[8,128]{1,0:T(8,128)S(1)}, f32[8,128]{1,0:T(8,128)S(1)}, u32[]{:S(2)}, u32[]{:S(2)}) collective-permute-start(f32[8,128]{1,0:T(8,128)S(1)} %get-tuple-element.22), channel_id=1, source_target_pairs={{0,1},{1,0},{2,3},{3,2},{4,5},{5,4},{6,7},{7,6},{8,9},{9,8},{10,11... | collective-permute-start | bytes 12296 | tf_op jit(solution)/shard_map/ppermute | solution.py:79
  43.1 3.0 %collective-permute-start.16 = (f32[8,128]{1,0:T(8,128)S(1)}, f32[8,128]{1,0:T(8,128)S(1)}, u32[]{:S(2)}, u32[]{:S(2)}) collective-permute-start(f32[8,128]{1,0:T(8,128)S(1)} %add.16), channel_id=1, source_target_pairs={{0,3},{1,2},{2,1},{3,0},{4,7},{5,6},{6,5},{7,4},{8,11},{9,10},{10,... | collective-permute-start | bytes 12296 | tf_op jit(solution)/shard_map/ppermute | solution.py:79

commit v3 on v2

--- a/solution.py
+++ b/solution.py
@@ -7,6 +7,7 @@
 from jax.experimental import pallas as pl
 from jax.experimental.pallas import tpu as pltpu
 from jax.sharding import PartitionSpec as P
+
 
 ITERS = 3
 
@@ -46,7 +47,7 @@
         ).astype(jnp.bfloat16)
 
     vectors = start_vectors
-    for iteration in range(ITERS):
+    for _ in range(ITERS):
         empty = jnp.zeros((vectors.shape[0], row_total), jnp.float32)
         sending = vectors.T.astype(jnp.bfloat16)
         v_piece = lax.all_gather(sending, "rows", axis=0, tiled=True)
@@ -74,13 +75,19 @@
     return vectors / (mean_abs[:, None] + 1e-06)
 
 
-def swap(value, axis, bit):
-    count = lax.axis_size(axis)
-    return lax.ppermute(value, axis, [(place, place ^ bit) for place in range(count)])
+def swap(value, row_bit, col_bit):
+    cols = lax.axis_size("cols")
+    count = lax.axis_size("rows") * cols
+    bits = row_bit * cols + col_bit
+    return lax.ppermute(value, ("rows", "cols"), [(place, place ^ bits) for place in range(count)])
 
 
 def call(body, outs, args, flops):
     moved = sum(a.size * a.dtype.itemsize for a in args)
+    return inner_call(body, outs, args, flops, moved)
+
+
+def inner_call(body, outs, args, flops, moved):
     return pl.pallas_call(
         body,
         out_shape=outs,
@@ -100,8 +107,16 @@
     )
 
 
-def pack(scale, p_ref, v_ref, d_ref, out_ref):
+def pack(scale, p_any, v_any, d_any, out_ref, p_ref, v_ref, d_ref, sems):
     span = p_ref.shape[0]
+    copies = [
+        pltpu.make_async_copy(source, target, sems.at[at])
+        for at, (source, target) in enumerate(((p_any, p_ref), (v_any, v_ref), (d_any, d_ref)))
+    ]
+    for copy in copies:
+        copy.start()
+    for copy in copies:
+        copy.wait()
     count = v_ref.shape[0]
     x = p_ref[...]
     f = x.astype(jnp.float32)
@@ -179,9 +194,9 @@
     part_ref[...] = dot(wide([r.vectors() for r in rows]), out_ref[...], 1, 0)
 
 
-def middle(scale, sa, sb, ka, kb, xa, xka, ya, xb, yb, part1, out_y, out_x, part_ref):
+def middle(scale, sa, sb, ka, kb, xa, xka, ya, xkb, yb, part1, out_y, out_x, part_ref):
     rows = pieces([sa, sb, ka, kb, xa, xka])
-    late = pieces([xb])
+    late = pieces([xkb])
     fill(scale, rows, pieces([yb]), out_y)
     fill(scale, late, pieces([sa, sb, ya, yb]), out_x)
     split = part1.shape[1]
@@ -190,8 +205,8 @@
     part_ref[:, split:] = dot(wide([r.vectors() for r in rows]), out_y[...], 1, 0) + part[:, split:]
 
 
-def last(scale, sa, sb, ya, yb, xkb, part2, out_k, part_ref):
-    late = pieces([xkb])
+def last(scale, sa, sb, ya, yb, xb, part2, out_k, part_ref):
+    late = pieces([xb])
     fill(scale, late, pieces([sa, sb, ya, yb]), out_k)
     part_ref[...] = part2[...] + dot(wide([r.vectors() for r in late]), out_k[...], 1, 0)
 
@@ -213,10 +228,10 @@
     out_ref[:, r2:] = dot(v, ak[...], 1, 1)
 
 
-def to_cols(sa, sb, ka, kb, xa, xka, xb, xkb, a1, ay, ax, ak, part, other, out_ref):
-    degree = wide([c.degree() for c in pieces([sa, sb, ka, kb, xa, xka, xb, xkb])])
+def to_cols(sa, sb, ka, kb, xa, xka, xkb, xb, a1, ay, ax, ak, part, other, out_ref):
+    degree = wide([c.degree() for c in pieces([sa, sb, ka, kb, xa, xka, xkb, xb])])
     block = degree.shape[1] // 8
-    state = (part[...] + order(other[...], (5, 7, 4, 6, 2, 0, 3, 1), block)) / degree
+    state = (part[...] + order(other[...], (5, 6, 4, 7, 2, 0, 1, 3), block)) / degree
     v = state.astype(jnp.bfloat16)
     split = a1.shape[1]
     r1 = a1.shape[0]
@@ -244,18 +259,24 @@
     def shape(rows, cols, kind=jnp.float32):
         return jax.ShapeDtypeStruct((rows, cols), kind)
 
-    message = call(
+    inputs = (points, start_vectors, degree[None, :])
+    message = pl.pallas_call(
         functools.partial(pack, scale),
-        shape(span + 8, features, jnp.bfloat16),
-        (points, start_vectors, degree[None, :]),
-        10**6,
-    )
-    remote = [swap(message, "rows", bit) for bit in range(2, row_count, 2)]
-    sa = jnp.stack([message, remote[0]])
-    sb = jnp.stack(remote[1:])
-    xa, ya, ka = swap(sa, "cols", 2), swap(sa, "rows", 1), swap(sa, "cols", 1)
-    xb, yb, kb = swap(sb, "cols", 2), swap(sb, "rows", 1), swap(sb, "cols", 1)
-    xka, xkb = swap(xa, "cols", 1), swap(xb, "cols", 1)
+        out_shape=shape(span + 8, features, jnp.bfloat16),
+        in_specs=[pl.BlockSpec(memory_space=pltpu.HBM)] * 3,
+        out_specs=pl.BlockSpec(memory_space=pltpu.VMEM),
+        scratch_shapes=[pltpu.VMEM(a.shape, a.dtype) for a in inputs]
+        + [pltpu.SemaphoreType.DMA((3,))],
+        compiler_params=pltpu.CompilerParams(vmem_limit_bytes=16 * 2**20),
+    )(*inputs)
+    z3 = swap(message, 6, 1)
+    z2 = swap(message, 4, 1)
+    z1 = swap(message, 2, 1)
+    sa = jnp.stack([message, z1])
+    sb = jnp.stack([z2, z3])
+    xka, ya, ka = swap(sa, 0, 3), swap(sa, 1, 1), swap(sa, 0, 1)
+    xkb, yb, kb = swap(sb, 0, 3), swap(sb, 1, 1), swap(sb, 0, 1)
+    xa, xb = swap(xka, 0, 1), swap(xkb, 0, 1)
 
     half = sa.shape[0] * span
     rest = sb.shape[0] * span
@@ -271,46 +292,48 @@
     ay, ax, part2 = call(
         functools.partial(middle, scale),
         (shape(r1, rest, jnp.bfloat16), shape(rest, width, jnp.bfloat16), shape(count, width)),
-        (sa, sb, ka, kb, xa, xka, ya, xb, yb, part1),
+        (sa, sb, ka, kb, xa, xka, ya, xkb, yb, part1),
         2 * features * (r1 * rest + rest * width),
     )
     ak, part = call(
         functools.partial(last, scale),
         (shape(rest, width, jnp.bfloat16), shape(count, width)),
-        (sa, sb, ya, yb, xkb, part2),
+        (sa, sb, ya, yb, xb, part2),
         2 * features * rest * width,
     )
     part = call(
         to_rows,
         shape(count, r1 + 2 * rest),
-        (sa, sb, ya, yb, a1, ay, ax, ak, part, swap(part, "rows", 1)),
+        (sa, sb, ya, yb, a1, ay, ax, ak, part, swap(part, 1, 1)),
         10**8,
     )
-    part = part + order(swap(part, "cols", 1), (2, 3, 0, 1, 5, 4, 7, 6), rest)
+    part = part + order(swap(part, 0, 1), (2, 3, 0, 1, 5, 4, 7, 6), rest)
     part = call(
         to_cols,
         shape(count, width),
-        (sa, sb, ka, kb, xa, xka, xb, xkb, a1, ay, ax, ak, part, swap(part, "cols", 3)),
+        (sa, sb, ka, kb, xa, xka, xkb, xb, a1, ay, ax, ak, part, swap(part, 0, 3)),
         10**8,
     )
     own, total = call(
         finish,
         (shape(count, span), shape(count, span)),
-        (sa, sb, ya, yb, part, swap(part, "rows", 1)),
+        (sa, sb, ya, yb, part, swap(part, 1, 1)),
         10**6,
     )
-    total = total + swap(total, "cols", 1)
-    total = total + swap(total, "cols", 3)
+    total = total + swap(total, 0, 1)
+    total = total + swap(total, 0, 3)
     mean_abs = total / (span * row_count * lax.axis_size("cols"))
     return own / (mean_abs + 1e-06)
 
 
 def solution(mesh):
-    small = mesh.shape["cols"] == 4 and mesh.shape["rows"] == 8
-    return jax.shard_map(
-        planes if small else general,
+    specs = dict(
         mesh=mesh,
         in_specs=(P(("rows", "cols"), None), P(None, ("rows", "cols")), P(("rows", "cols"))),
         out_specs=P(None, ("rows", "cols")),
         check_vma=False,
     )
+    if mesh.shape["cols"] != 4 or mesh.shape["rows"] != 8:
+        return jax.shard_map(general, **specs)
+
+    return jax.shard_map(planes, **specs)

time: 46.9 us -> 46 us (0.981)
  waiting for transfers between devices: 21 us -> 19.7 us
    ppermute x17, waiting for transfers between devices: 21 us -> 19.7 us  [swap(): lax.ppermute(value, ('rows', 'cols'), [(place, place ^ bits) for place in...]
where the time goes in v3:
time: 46 us; the launch traced here: 45.8 us
  waiting for transfers between devices  19.7 us (43%)
  starting transfers between devices  16.6 us (36%)
  Pallas kernels  6.53 us (14%)
  local copies, waits for them, and re-layouts  2.19 us (5%)
  other arithmetic  0.65 us (1%)
    ppermute x17, waiting for transfers between devices, swap(): lax.ppermute(value, ('rows', 'cols'), [(place, place ^ bits) for place in...  19.7 us
    ppermute x17, starting transfers between devices, swap(): lax.ppermute(value, ('rows', 'cols'), [(place, place ^ bits) for place in...  16.6 us
    pallas_call x6, Pallas kernels, inner_call(): pl.pallas_call(body, out_shape=outs, in_specs=[pl.BlockSpec(memory_space=...  6.28 us
    unnamed x11, local copies, waits for them, and re-layouts  2.19 us
  transfers between devices with their start and end apart: 17, of which 11 were waited for; matrix products, arithmetic and copies ran while one was open for 0% of the time, Pallas kernels for 8%

profile of v3, /device:TPU:0, one launch (start us, length us, event | category | flops | bytes accessed | tf_op | source)
XLA Modules:
  0.0 45.8 jit_solution(13311716820060982057)
XLA Ops:
  0.0 0.8 %copy-done = bf16[128,256]{1,0:T(8,128)(2,1)S(1)} copy-done((bf16[128,256]{1,0:T(8,128)(2,1)S(1)}, bf16[128,256]{1,0:T(8,128)(2,1)}, u32[]{:S(2)}) %copy-start) | copy-done | bytes 65560
  0.8 0.7 %copy-done.1 = f32[8,128]{1,0:T(8,128)S(1)} copy-done((f32[8,128]{1,0:T(8,128)S(1)}, f32[8,128]{1,0:T(8,128)}, u32[]{:S(2)}) %copy-start.1) | copy-done | bytes 4120
  1.5 0.7 %copy-done.2 = bf16[128]{0:T(256)(128)(2,1)S(1)} copy-done((bf16[128]{0:T(256)(128)(2,1)S(1)}, bf16[128]{0:T(256)(128)(2,1)}, u32[]{:S(2)}) %copy-start.2) | copy-done | bytes 280
  2.4 2.6 %collective-permute-start = (bf16[136,256]{1,0:T(8,128)(2,1)S(1)}, bf16[136,256]{1,0:T(8,128)(2,1)S(1)}, u32[]{:S(2)}, u32[]{:S(2)}) collective-permute-start(bf16[136,256]{1,0:T(8,128)(2,1)S(1)} %shard_map.37), channel_id=1, source_target_pairs={{0,9},{1,8},{2,11},{3,10},{4,13},{5,12},{6,15},{7,14},{8,1},{9,0},... | collective-permute-start | bytes 208904 | tf_op jit(solution)/shard_map/ppermute | solution.py:82
  5.0 2.8 %collective-permute-start.2 = (bf16[136,256]{1,0:T(8,128)(2,1)S(1)}, bf16[136,256]{1,0:T(8,128)(2,1)S(1)}, u32[]{:S(2)}, u32[]{:S(2)}) collective-permute-start(bf16[136,256]{1,0:T(8,128)(2,1)S(1)} %shard_map.37), channel_id=1, source_target_pairs={{0,25},{1,24},{2,27},{3,26},{4,29},{5,28},{6,31},{7,30},{8,17},{9,... | collective-permute-start | bytes 208904 | tf_op jit(solution)/shard_map/ppermute | solution.py:82
  7.9 1.7 %collective-permute-start.7 = (bf16[2,136,256]{2,1,0:T(8,128)(2,1)S(1)}, bf16[2,136,256]{2,1,0:T(8,128)(2,1)S(1)}, u32[]{:S(2)}, u32[]{:S(2)}) collective-permute-start(bf16[2,136,256]{2,1,0:T(8,128)(2,1)S(1)} %pad_maximum_fusion.sa), channel_id=1, source_target_pairs={{0,3},{1,2},{2,1},{3,0},{4,7},{5,6},{6,5},{7,4},{8,11},{9,10},{10,... | collective-permute-start | bytes 417800 | tf_op jit(solution)/shard_map/ppermute | solution.py:82
  10.0 1.9 %collective-permute-done.2 = bf16[136,256]{1,0:T(8,128)(2,1)S(1)} collective-permute-done((bf16[136,256]{1,0:T(8,128)(2,1)S(1)}, bf16[136,256]{1,0:T(8,128)(2,1)S(1)}, u32[]{:S(2)}, u32[]{:S(2)}) %collective-permute-start.2) | collective-permute-done | bytes 69664 | tf_op jit(solution)/shard_map/ppermute | solution.py:82
  11.9 3.1 %collective-permute-done.1 = bf16[136,256]{1,0:T(8,128)(2,1)S(1)} collective-permute-done((bf16[136,256]{1,0:T(8,128)(2,1)S(1)}, bf16[136,256]{1,0:T(8,128)(2,1)S(1)}, u32[]{:S(2)}, u32[]{:S(2)}) %collective-permute-start.1) | collective-permute-done | bytes 69664 | tf_op jit(solution)/shard_map/ppermute | solution.py:82
  15.1 1.3 %collective-permute-start.9 = (bf16[2,136,256]{2,1,0:T(8,128)(2,1)S(1)}, bf16[2,136,256]{2,1,0:T(8,128)(2,1)S(1)}, u32[]{:S(2)}, u32[]{:S(2)}) collective-permute-start(bf16[2,136,256]{2,1,0:T(8,128)(2,1)S(1)} %pad_maximum_fusion.1.sb), channel_id=1, source_target_pairs={{0,3},{1,2},{2,1},{3,0},{4,7},{5,6},{6,5},{7,4},{8,11},{9,10},{10,... | collective-permute-start | bytes 417800 | tf_op jit(solution)/shard_map/ppermute | solution.py:82
  16.4 1.5 %collective-permute-start.3 = (bf16[2,136,256]{2,1,0:T(8,128)(2,1)S(1)}, bf16[2,136,256]{2,1,0:T(8,128)(2,1)S(1)}, u32[]{:S(2)}, u32[]{:S(2)}) collective-permute-start(bf16[2,136,256]{2,1,0:T(8,128)(2,1)S(1)} %pad_maximum_fusion.sa), channel_id=1, source_target_pairs={{0,5},{1,4},{2,7},{3,6},{4,1},{5,0},{6,3},{7,2},{8,13},{9,12},{10,... | collective-permute-start | bytes 417800 | tf_op jit(solution)/shard_map/ppermute | solution.py:82
  18.0 0.4 collective-permute-start.8
  18.6 2.2 %collective-permute-done.9.xkb = bf16[2,136,256]{2,1,0:T(8,128)(2,1)S(1)} collective-permute-done((bf16[2,136,256]{2,1,0:T(8,128)(2,1)S(1)}, bf16[2,136,256]{2,1,0:T(8,128)(2,1)S(1)}, u32[]{:S(2)}, u32[]{:S(2)}) %collective-permute-start.9) | collective-permute-done | bytes 139296 | tf_op jit(solution)/shard_map/ppermute | solution.py:82
  20.8 0.4 collective-permute-start.10
  21.2 0.7 %collective-permute-done.3.ya = bf16[2,136,256]{2,1,0:T(8,128)(2,1)S(1)} collective-permute-done((bf16[2,136,256]{2,1,0:T(8,128)(2,1)S(1)}, bf16[2,136,256]{2,1,0:T(8,128)(2,1)S(1)}, u32[]{:S(2)}, u32[]{:S(2)}) %collective-permute-start.3) | collective-permute-done | bytes 139296 | tf_op jit(solution)/shard_map/ppermute | solution.py:82
  22.0 2.2 %shard_map.38 = (bf16[1536,768]{1,0:T(8,128)(2,1)S(1)}, f32[8,768]{1,0:T(8,128)S(1)}) custom-call(bf16[2,136,256]{2,1,0:T(8,128)(2,1)S(1)} %pad_maximum_fusion.sa, bf16[2,136,256]{2,1,0:T(8,128)(2,1)S(1)} %pad_maximum_fusion.1.sb, bf16[2,136,256]{2,1,0:T(8,128)(2,1)S(1)} %collective-permute-done.5.ka, bf16[2,136,256]{2,1,0:T(8,128)(2,1)S(1)} %collective-permute-done.6.kb, ...), custom_call_target="tpu_custom_call" | custom-call | flops 603979776 | bytes 974848 | tf_op jit(solution)/shard_map/pallas_call | solution.py:91
  24.2 0.6 %collective-permute-done.4.yb = bf16[2,136,256]{2,1,0:T(8,128)(2,1)S(1)} collective-permute-done((bf16[2,136,256]{2,1,0:T(8,128)(2,1)S(1)}, bf16[2,136,256]{2,1,0:T(8,128)(2,1)S(1)}, u32[]{:S(2)}, u32[]{:S(2)}) %collective-permute-start.4) | collective-permute-done | bytes 139296 | tf_op jit(solution)/shard_map/ppermute | solution.py:82
  24.7 1.5 %shard_map.39 = (bf16[1536,256]{1,0:T(8,128)(2,1)S(1)}, bf16[256,1024]{1,0:T(8,128)(2,1)S(1)}, f32[8,1024]{1,0:T(8,128)S(1)}) custom-call(bf16[2,136,256]{2,1,0:T(8,128)(2,1)S(1)} %pad_maximum_fusion.sa, bf16[2,136,256]{2,1,0:T(8,128)(2,1)S(1)} %pad_maximum_fusion.1.sb, bf16[2,136,256]{2,1,0:T(8,128)(2,1)S(1)} %collective-permute-done.5.ka, ...), custom_call_target="tpu_custom_call" | custom-call | flops 335544320 | bytes 1277952 | tf_op jit(solution)/shard_map/pallas_call | solution.py:91
  26.2 0.7 %shard_map.40 = (bf16[256,1024]{1,0:T(8,128)(2,1)S(1)}, f32[8,1024]{1,0:T(8,128)S(1)}) custom-call(bf16[2,136,256]{2,1,0:T(8,128)(2,1)S(1)} %pad_maximum_fusion.sa, bf16[2,136,256]{2,1,0:T(8,128)(2,1)S(1)} %pad_maximum_fusion.1.sb, bf16[2,136,256]{2,1,0:T(8,128)(2,1)S(1)} %collective-permute-done.3.ya, bf16[2,136,256]{2,1,0:T(8,128)(2,1)S(1)} %collective-permute-done.4.yb, ...), custom_call_target="tpu_custom_call" | custom-call | flops 134217728 | bytes 729088 | tf_op jit(solution)/shard_map/pallas_call | solution.py:91
  26.9 1.7 %collective-permute-start.11 = (f32[8,1024]{1,0:T(8,128)S(1)}, f32[8,1024]{1,0:T(8,128)S(1)}, u32[]{:S(2)}, u32[]{:S(2)}) collective-permute-start(f32[8,1024]{1,0:T(8,128)S(1)} %get-tuple-element.20.part), channel_id=1, source_target_pairs={{0,5},{1,4},{2,7},{3,6},{4,1},{5,0},{6,3},{7,2},{8,13},{9,12},{10,... | collective-permute-start | bytes 98312 | tf_op jit(solution)/shard_map/ppermute | solution.py:82
  28.6 1.7 %collective-permute-done.11.other = f32[8,1024]{1,0:T(8,128)S(1)} collective-permute-done((f32[8,1024]{1,0:T(8,128)S(1)}, f32[8,1024]{1,0:T(8,128)S(1)}, u32[]{:S(2)}, u32[]{:S(2)}) %collective-permute-start.11) | collective-permute-done | bytes 32800 | tf_op jit(solution)/shard_map/ppermute | solution.py:82
  30.2 1.2 %shard_map.41 = f32[8,2048]{1,0:T(8,128)S(1)} custom-call(bf16[2,136,256]{2,1,0:T(8,128)(2,1)S(1)} %pad_maximum_fusion.sa, bf16[2,136,256]{2,1,0:T(8,128)(2,1)S(1)} %pad_maximum_fusion.1.sb, bf16[2,136,256]{2,1,0:T(8,128)(2,1)S(1)} %collective-permute-done.3.ya, bf16[2,136,256]{2,1,0:T(8,128)(2,1)S(1)} %collective-permute-done.4.yb, ...), custom_call_target="tpu_custom_call" | custom-call | flops 100000000 | bytes 4816896 | tf_op jit(solution)/shard_map/pallas_call | solution.py:91
  31.4 0.5 %collective-permute-start.12 = (f32[8,2048]{1,0:T(8,128)S(1)}, f32[8,2048]{1,0:T(8,128)S(1)}, u32[]{:S(2)}, u32[]{:S(2)}) collective-permute-start(f32[8,2048]{1,0:T(8,128)S(1)} %shard_map.41), channel_id=1, source_target_pairs={{0,1},{1,0},{2,3},{3,2},{4,5},{5,4},{6,7},{7,6},{8,9},{9,8},{10,11... | collective-permute-start | bytes 196616 | tf_op jit(solution)/shard_map/ppermute | solution.py:82
  32.0 0.9 %collective-permute-done.12 = f32[8,2048]{1,0:T(8,128)S(1)} collective-permute-done((f32[8,2048]{1,0:T(8,128)S(1)}, f32[8,2048]{1,0:T(8,128)S(1)}, u32[]{:S(2)}, u32[]{:S(2)}) %collective-permute-start.12) | collective-permute-done | bytes 65568 | tf_op jit(solution)/shard_map/ppermute | solution.py:82
  32.9 0.6 %collective-permute-start.13 = (f32[8,2048]{1,0:T(8,128)S(1)}, f32[8,2048]{1,0:T(8,128)S(1)}, u32[]{:S(2)}, u32[]{:S(2)}) collective-permute-start(f32[8,2048]{1,0:T(8,128)S(1)} %add.15.part), channel_id=1, source_target_pairs={{0,3},{1,2},{2,1},{3,0},{4,7},{5,6},{6,5},{7,4},{8,11},{9,10},{10,... | collective-permute-start | bytes 196616 | tf_op jit(solution)/shard_map/ppermute | solution.py:82
  33.5 3.4 %collective-permute-done.13.other = f32[8,2048]{1,0:T(8,128)S(1)} collective-permute-done((f32[8,2048]{1,0:T(8,128)S(1)}, f32[8,2048]{1,0:T(8,128)S(1)}, u32[]{:S(2)}, u32[]{:S(2)}) %collective-permute-start.13) | collective-permute-done | bytes 65568 | tf_op jit(solution)/shard_map/ppermute | solution.py:82
  36.8 0.6 %shard_map.42.part = f32[8,1024]{1,0:T(8,128)S(1)} custom-call(bf16[2,136,256]{2,1,0:T(8,128)(2,1)S(1)} %pad_maximum_fusion.sa, bf16[2,136,256]{2,1,0:T(8,128)(2,1)S(1)} %pad_maximum_fusion.1.sb, bf16[2,136,256]{2,1,0:T(8,128)(2,1)S(1)} %collective-permute-done.5.ka, bf16[2,136,256]{2,1,0:T(8,128)(2,1)S(1)} %collective-permute-done.6.kb, ...), custom_call_target="tpu_custom_call" | custom-call | flops 100000000 | bytes 5439488 | tf_op jit(solution)/shard_map/pallas_call | solution.py:91
  37.5 1.5 %collective-permute-start.14 = (f32[8,1024]{1,0:T(8,128)S(1)}, f32[8,1024]{1,0:T(8,128)S(1)}, u32[]{:S(2)}, u32[]{:S(2)}) collective-permute-start(f32[8,1024]{1,0:T(8,128)S(1)} %shard_map.42.part), channel_id=1, source_target_pairs={{0,5},{1,4},{2,7},{3,6},{4,1},{5,0},{6,3},{7,2},{8,13},{9,12},{10,... | collective-permute-start | bytes 98312 | tf_op jit(solution)/shard_map/ppermute | solution.py:82
  39.0 1.9 %collective-permute-done.14.other = f32[8,1024]{1,0:T(8,128)S(1)} collective-permute-done((f32[8,1024]{1,0:T(8,128)S(1)}, f32[8,1024]{1,0:T(8,128)S(1)}, u32[]{:S(2)}, u32[]{:S(2)}) %collective-permute-start.14) | collective-permute-done | bytes 32800 | tf_op jit(solution)/shard_map/ppermute | solution.py:82
  41.3 0.8 %collective-permute-done.15 = f32[8,128]{1,0:T(8,128)S(1)} collective-permute-done((f32[8,128]{1,0:T(8,128)S(1)}, f32[8,128]{1,0:T(8,128)S(1)}, u32[]{:S(2)}, u32[]{:S(2)}) %collective-permute-start.15) | collective-permute-done | bytes 4128 | tf_op jit(solution)/shard_map/ppermute | solution.py:82
  42.1 0.5 %collective-permute-start.16 = (f32[8,128]{1,0:T(8,128)S(1)}, f32[8,128]{1,0:T(8,128)S(1)}, u32[]{:S(2)}, u32[]{:S(2)}) collective-permute-start(f32[8,128]{1,0:T(8,128)S(1)} %add.16), channel_id=1, source_target_pairs={{0,3},{1,2},{2,1},{3,0},{4,7},{5,6},{6,5},{7,4},{8,11},{9,10},{10,... | collective-permute-start | bytes 12296 | tf_op jit(solution)/shard_map/ppermute | solution.py:82
  42.6 2.6 %collective-permute-done.16 = f32[8,128]{1,0:T(8,128)S(1)} collective-permute-done((f32[8,128]{1,0:T(8,128)S(1)}, f32[8,128]{1,0:T(8,128)S(1)}, u32[]{:S(2)}, u32[]{:S(2)}) %collective-permute-start.16) | collective-permute-done | bytes 4128 | tf_op jit(solution)/shard_map/ppermute | solution.py:82
  45.2 0.6 %add_divide_fusion = f32[8,128]{1,0:T(8,128)} fusion(f32[8,128]{1,0:T(8,128)S(1)} %get-tuple-element.21, f32[8,128]{1,0:T(8,128)S(1)} %add.16, f32[8,128]{1,0:T(8,128)S(1)} %collective-permute-done.16), kind=kLoop, calls=%fused_computation.8 | loop fusion | flops 4096 | bytes 16384 | tf_op jit(solution)/shard_map/div | solution.py:326
  (26 shorter events, 1.6 us)
Async XLA Ops:
  0.0 0.8 %copy-start = (bf16[128,256]{1,0:T(8,128)(2,1)S(1)}, bf16[128,256]{1,0:T(8,128)(2,1)}, u32[]{:S(2)}) copy-start(bf16[128,256]{1,0:T(8,128)(2,1)} %p_any.1) | copy-start | bytes 196612
  0.8 0.7 %copy-start.1 = (f32[8,128]{1,0:T(8,128)S(1)}, f32[8,128]{1,0:T(8,128)}, u32[]{:S(2)}) copy-start(f32[8,128]{1,0:T(8,128)} %v_any.1) | copy-start | bytes 12292
  1.5 0.7 %copy-start.2 = (bf16[128]{0:T(256)(128)(2,1)S(1)}, bf16[128]{0:T(256)(128)(2,1)}, u32[]{:S(2)}) copy-start(bf16[128]{0:T(256)(128)(2,1)} %param.5) | copy-start | bytes 772
  2.4 5.4 %collective-permute-start = (bf16[136,256]{1,0:T(8,128)(2,1)S(1)}, bf16[136,256]{1,0:T(8,128)(2,1)S(1)}, u32[]{:S(2)}, u32[]{:S(2)}) collective-permute-start(bf16[136,256]{1,0:T(8,128)(2,1)S(1)} %shard_map.37), channel_id=1, source_target_pairs={{0,9},{1,8},{2,11},{3,10},{4,13},{5,12},{6,15},{7,14},{8,1},{9,0},... | collective-permute-start | bytes 208904 | tf_op jit(solution)/shard_map/ppermute | solution.py:82
  5.0 6.9 %collective-permute-start.2 = (bf16[136,256]{1,0:T(8,128)(2,1)S(1)}, bf16[136,256]{1,0:T(8,128)(2,1)S(1)}, u32[]{:S(2)}, u32[]{:S(2)}) collective-permute-start(bf16[136,256]{1,0:T(8,128)(2,1)S(1)} %shard_map.37), channel_id=1, source_target_pairs={{0,25},{1,24},{2,27},{3,26},{4,29},{5,28},{6,31},{7,30},{8,17},{9,... | collective-permute-start | bytes 208904 | tf_op jit(solution)/shard_map/ppermute | solution.py:82
  7.8 7.3 %collective-permute-start.1 = (bf16[136,256]{1,0:T(8,128)(2,1)S(1)}, bf16[136,256]{1,0:T(8,128)(2,1)S(1)}, u32[]{:S(2)}, u32[]{:S(2)}) collective-permute-start(bf16[136,256]{1,0:T(8,128)(2,1)S(1)} %shard_map.37), channel_id=1, source_target_pairs={{0,17},{1,16},{2,19},{3,18},{4,21},{5,20},{6,23},{7,22},{8,25},{9,... | collective-permute-start | bytes 208904 | tf_op jit(solution)/shard_map/ppermute | solution.py:82
  7.9 10.1 %collective-permute-start.7 = (bf16[2,136,256]{2,1,0:T(8,128)(2,1)S(1)}, bf16[2,136,256]{2,1,0:T(8,128)(2,1)S(1)}, u32[]{:S(2)}, u32[]{:S(2)}) collective-permute-start(bf16[2,136,256]{2,1,0:T(8,128)(2,1)S(1)} %pad_maximum_fusion.sa), channel_id=1, source_target_pairs={{0,3},{1,2},{2,1},{3,0},{4,7},{5,6},{6,5},{7,4},{8,11},{9,10},{10,... | collective-permute-start | bytes 417800 | tf_op jit(solution)/shard_map/ppermute | solution.py:82
  9.6 8.8 %collective-permute-start.5 = (bf16[2,136,256]{2,1,0:T(8,128)(2,1)S(1)}, bf16[2,136,256]{2,1,0:T(8,128)(2,1)S(1)}, u32[]{:S(2)}, u32[]{:S(2)}) collective-permute-start(bf16[2,136,256]{2,1,0:T(8,128)(2,1)S(1)} %pad_maximum_fusion.sa), channel_id=1, source_target_pairs={{0,1},{1,0},{2,3},{3,2},{4,5},{5,4},{6,7},{7,6},{8,9},{9,8},{10,11... | collective-permute-start | bytes 417800 | tf_op jit(solution)/shard_map/ppermute | solution.py:82
  15.1 5.7 %collective-permute-start.9 = (bf16[2,136,256]{2,1,0:T(8,128)(2,1)S(1)}, bf16[2,136,256]{2,1,0:T(8,128)(2,1)S(1)}, u32[]{:S(2)}, u32[]{:S(2)}) collective-permute-start(bf16[2,136,256]{2,1,0:T(8,128)(2,1)S(1)} %pad_maximum_fusion.1.sb), channel_id=1, source_target_pairs={{0,3},{1,2},{2,1},{3,0},{4,7},{5,6},{6,5},{7,4},{8,11},{9,10},{10,... | collective-permute-start | bytes 417800 | tf_op jit(solution)/shard_map/ppermute | solution.py:82
  16.4 5.6 %collective-permute-start.3 = (bf16[2,136,256]{2,1,0:T(8,128)(2,1)S(1)}, bf16[2,136,256]{2,1,0:T(8,128)(2,1)S(1)}, u32[]{:S(2)}, u32[]{:S(2)}) collective-permute-start(bf16[2,136,256]{2,1,0:T(8,128)(2,1)S(1)} %pad_maximum_fusion.sa), channel_id=1, source_target_pairs={{0,5},{1,4},{2,7},{3,6},{4,1},{5,0},{6,3},{7,2},{8,13},{9,12},{10,... | collective-permute-start | bytes 417800 | tf_op jit(solution)/shard_map/ppermute | solution.py:82
  17.9 4.1 %collective-permute-start.6 = (bf16[2,136,256]{2,1,0:T(8,128)(2,1)S(1)}, bf16[2,136,256]{2,1,0:T(8,128)(2,1)S(1)}, u32[]{:S(2)}, u32[]{:S(2)}) collective-permute-start(bf16[2,136,256]{2,1,0:T(8,128)(2,1)S(1)} %pad_maximum_fusion.1.sb), channel_id=1, source_target_pairs={{0,1},{1,0},{2,3},{3,2},{4,5},{5,4},{6,7},{7,6},{8,9},{9,8},{10,11... | collective-permute-start | bytes 417800 | tf_op jit(solution)/shard_map/ppermute | solution.py:82
  18.0 3.9 %collective-permute-start.8 = (bf16[2,136,256]{2,1,0:T(8,128)(2,1)S(1)}, bf16[2,136,256]{2,1,0:T(8,128)(2,1)S(1)}, u32[]{:S(2)}, u32[]{:S(2)}) collective-permute-start(bf16[2,136,256]{2,1,0:T(8,128)(2,1)S(1)} %collective-permute-done.7.xka), channel_id=1, source_target_pairs={{0,1},{1,0},{2,3},{3,2},{4,5},{5,4},{6,7},{7,6},{8,9},{9,8},{10,11... | collective-permute-start | bytes 417800 | tf_op jit(solution)/shard_map/ppermute | solution.py:82
  18.4 6.3 %collective-permute-start.4 = (bf16[2,136,256]{2,1,0:T(8,128)(2,1)S(1)}, bf16[2,136,256]{2,1,0:T(8,128)(2,1)S(1)}, u32[]{:S(2)}, u32[]{:S(2)}) collective-permute-start(bf16[2,136,256]{2,1,0:T(8,128)(2,1)S(1)} %pad_maximum_fusion.1.sb), channel_id=1, source_target_pairs={{0,5},{1,4},{2,7},{3,6},{4,1},{5,0},{6,3},{7,2},{8,13},{9,12},{10,... | collective-permute-start | bytes 417800 | tf_op jit(solution)/shard_map/ppermute | solution.py:82
  20.8 5.4 %collective-permute-start.10 = (bf16[2,136,256]{2,1,0:T(8,128)(2,1)S(1)}, bf16[2,136,256]{2,1,0:T(8,128)(2,1)S(1)}, u32[]{:S(2)}, u32[]{:S(2)}) collective-permute-start(bf16[2,136,256]{2,1,0:T(8,128)(2,1)S(1)} %collective-permute-done.9.xkb), channel_id=1, source_target_pairs={{0,1},{1,0},{2,3},{3,2},{4,5},{5,4},{6,7},{7,6},{8,9},{9,8},{10,11... | collective-permute-start | bytes 417800 | tf_op jit(solution)/shard_map/ppermute | solution.py:82
  26.9 3.4 %collective-permute-start.11 = (f32[8,1024]{1,0:T(8,128)S(1)}, f32[8,1024]{1,0:T(8,128)S(1)}, u32[]{:S(2)}, u32[]{:S(2)}) collective-permute-start(f32[8,1024]{1,0:T(8,128)S(1)} %get-tuple-element.20.part), channel_id=1, source_target_pairs={{0,5},{1,4},{2,7},{3,6},{4,1},{5,0},{6,3},{7,2},{8,13},{9,12},{10,... | collective-permute-start | bytes 98312 | tf_op jit(solution)/shard_map/ppermute | solution.py:82
  31.4 1.4 %collective-permute-start.12 = (f32[8,2048]{1,0:T(8,128)S(1)}, f32[8,2048]{1,0:T(8,128)S(1)}, u32[]{:S(2)}, u32[]{:S(2)}) collective-permute-start(f32[8,2048]{1,0:T(8,128)S(1)} %shard_map.41), channel_id=1, source_target_pairs={{0,1},{1,0},{2,3},{3,2},{4,5},{5,4},{6,7},{7,6},{8,9},{9,8},{10,11... | collective-permute-start | bytes 196616 | tf_op jit(solution)/shard_map/ppermute | solution.py:82
  32.9 3.9 %collective-permute-start.13 = (f32[8,2048]{1,0:T(8,128)S(1)}, f32[8,2048]{1,0:T(8,128)S(1)}, u32[]{:S(2)}, u32[]{:S(2)}) collective-permute-start(f32[8,2048]{1,0:T(8,128)S(1)} %add.15.part), channel_id=1, source_target_pairs={{0,3},{1,2},{2,1},{3,0},{4,7},{5,6},{6,5},{7,4},{8,11},{9,10},{10,... | collective-permute-start | bytes 196616 | tf_op jit(solution)/shard_map/ppermute | solution.py:82
  37.5 3.4 %collective-permute-start.14 = (f32[8,1024]{1,0:T(8,128)S(1)}, f32[8,1024]{1,0:T(8,128)S(1)}, u32[]{:S(2)}, u32[]{:S(2)}) collective-permute-start(f32[8,1024]{1,0:T(8,128)S(1)} %shard_map.42.part), channel_id=1, source_target_pairs={{0,5},{1,4},{2,7},{3,6},{4,1},{5,0},{6,3},{7,2},{8,13},{9,12},{10,... | collective-permute-start | bytes 98312 | tf_op jit(solution)/shard_map/ppermute | solution.py:82
  40.9 1.2 %collective-permute-start.15 = (f32[8,128]{1,0:T(8,128)S(1)}, f32[8,128]{1,0:T(8,128)S(1)}, u32[]{:S(2)}, u32[]{:S(2)}) collective-permute-start(f32[8,128]{1,0:T(8,128)S(1)} %get-tuple-element.22), channel_id=1, source_target_pairs={{0,1},{1,0},{2,3},{3,2},{4,5},{5,4},{6,7},{7,6},{8,9},{9,8},{10,11... | collective-permute-start | bytes 12296 | tf_op jit(solution)/shard_map/ppermute | solution.py:82
  42.1 3.0 %collective-permute-start.16 = (f32[8,128]{1,0:T(8,128)S(1)}, f32[8,128]{1,0:T(8,128)S(1)}, u32[]{:S(2)}, u32[]{:S(2)}) collective-permute-start(f32[8,128]{1,0:T(8,128)S(1)} %add.16), channel_id=1, source_target_pairs={{0,3},{1,2},{2,1},{3,0},{4,7},{5,6},{6,5},{7,4},{8,11},{9,10},{10,... | collective-permute-start | bytes 12296 | tf_op jit(solution)/shard_map/ppermute | solution.py:82
